TPU v7x, 32 devices: a whole 2x2x4 slice. The times are simulated.
32 devices in a mesh: gx: 8 (over y, x, core), gy: 4 (over z).
Axes of the slice: x: 2, y: 2, z: 4, core: 2. Of those that a mesh axis runs over, the one named last changes fastest.
Arguments:
- source: float32 [160, 80, 640], P('gx', 'gy'), may hold values from -210 to 210
- conductivity: float32 [160, 80, 640], P('gx', 'gy'), may hold values from 0.001 to 1
- absorption: float32 [160, 80, 640], P('gx', 'gy'), may hold values from 1 to 10
Outputs:
- solution: float32 [160, 80, 640], P('gx', 'gy')
- correction: float32 [96, 48, 384], P('gx', 'gy')
All inputs are finite; a program needn't handle non-finite values.
Results may differ from a plain program's by a relative error of at most 0.00023.
Values sent between devices are 32-bit elements; how exact they have to be, the bound alone decides.
A program may use at most 128 MiB of HBM per device.

v0:
```python
import functools
import math

import jax
import jax.numpy as jnp
import numpy as np
from jax import lax
from jax.experimental import pallas as pl
from jax.experimental.pallas import tpu as pltpu
from jax.sharding import PartitionSpec as P

SWEEPS = 3
STAGES = 10
MESH = pl.DeviceIdType.MESH
DIRS = [(-1, 0), (1, 0), (0, -1), (0, 1), (-1, -1), (-1, 1), (1, -1), (1, 1)]


def deriv_table(points):
    count = len(points)
    barycentric = np.array(
        [
            1.0 / np.prod([points[j] - points[k] for k in range(count) if k != j])
            for j in range(count)
        ]
    )
    table = np.zeros((count, count))
    for i in range(count):
        for j in range(count):
            if i != j:
                table[i, j] = barycentric[j] / (barycentric[i] * (points[i] - points[j]))
        table[i, i] = -np.sum(table[i])
    return table


ROOT = math.sqrt(3.0 / 7.0)
FINE_POINTS = np.array([-1.0, -ROOT, 0.0, ROOT, 1.0])
FINE_W = np.array([0.1, 49.0 / 90.0, 32.0 / 45.0, 49.0 / 90.0, 0.1])
COARSE_POINTS = np.array([-1.0, 0.0, 1.0])
COARSE_W = np.array([1.0 / 3.0, 4.0 / 3.0, 1.0 / 3.0])
FINE_D = deriv_table(FINE_POINTS)
COARSE_D = deriv_table(COARSE_POINTS)
INTERP = np.stack(
    [
        FINE_POINTS * (FINE_POINTS - 1.0) / 2.0,
        1.0 - FINE_POINTS**2,
        FINE_POINTS * (FINE_POINTS + 1.0) / 2.0,
    ],
    1,
)
RESTRICT = INTERP.T * np.array([0.5, 1.0, 1.0, 1.0, 0.5])[None, :]
QF, QC = 5, 3


def chebyshev_coefficients():
    theta, delta, sigma, rho = 0.75, 0.45, 5.0 / 3.0, 0.6
    x = np.zeros(SWEEPS + 1)
    r = np.zeros(SWEEPS + 1)
    r[0] = 1.0
    d = r / theta
    for sweep in range(SWEEPS):
        x = x + d
        r = r - np.concatenate([[0.0], d[:-1]])
        if sweep + 1 < SWEEPS:
            rho_next = 1.0 / (2.0 * sigma - rho)
            d = rho_next * rho * d + 2.0 * rho_next / delta * r
            rho = rho_next
    return [float(v) for v in x[:SWEEPS]]


CHEB = chebyshev_coefficients()


def antisym(table, u):
    n = len(u)
    half = n // 2
    even = [u[j] + u[n - 1 - j] for j in range(half)]
    odd = [u[j] - u[n - 1 - j] for j in range(half)]
    out = [None] * n
    for i in range(half):
        p = float(table[i, half]) * u[half]
        q = None
        for j in range(half):
            s = (table[i, j] + table[i, n - 1 - j]) / 2
            t = (table[i, j] - table[i, n - 1 - j]) / 2
            p = p + float(s) * even[j]
            q = float(t) * odd[j] if q is None else q + float(t) * odd[j]
        out[i] = q + p
        out[n - 1 - i] = q - p
    mid = None
    for j in range(half):
        term = float(table[half, j]) * odd[j]
        mid = term if mid is None else mid + term
    out[half] = mid
    return out


def dense(table, u):
    out = []
    for i in range(table.shape[0]):
        acc = None
        for j in range(table.shape[1]):
            c = float(table[i, j])
            if abs(c) < 1e-14:
                continue
            term = u[j] if c == 1.0 else c * u[j]
            acc = term if acc is None else acc + term
        out.append(acc)
    return out


def plane_starts(q, axis, a, b):
    strides = (q * q, q, 1)
    other = [s for k, s in enumerate(strides) if k != axis]
    return a * other[0] + b * other[1], strides[axis]


def z_sum(line, lanes):
    lo, hi = line[0], line[-1]
    line[-1] = hi + pltpu.roll(lo, lanes - 1, 1)
    line[0] = lo + pltpu.roll(hi, 1, 1)
    return line


def local_op(src, dst, flux, mass, table, lanes):
    q = table.shape[0]
    for axis in range(3):

        @pl.loop(0, q)
        def _(a, axis=axis):
            def read(b):
                start, step = plane_starts(q, axis, a, b)
                u = [src[start + step * i] for i in range(q)]
                base = None if axis == 0 else [dst[start + step * i] for i in range(q)]
                return u, base

            ahead = read(0)
            for b in range(q):
                u, base = ahead
                if b + 1 < q:
                    ahead = read(b + 1)
                start, step = plane_starts(q, axis, a, b)
                g = antisym(table, u)
                g = [flux[start + step * i] * g[i] for i in range(q)]
                r = antisym(table.T, g)
                for i in range(q):
                    r[i] = (mass[start + step * i] * u[i] if base is None else base[i]) + r[i]
                if axis == 2:
                    r = z_sum(r, lanes)
                for i in range(q):
                    dst[start + step * i] = r[i]


def local_diag(dst, flux, mass, table, lanes):
    q = table.shape[0]
    square = (table * table).T
    for axis in range(3):

        @pl.loop(0, q)
        def _(a, axis=axis):
            for b in range(q):
                start, step = plane_starts(q, axis, a, b)
                r = dense(square, [flux[start + step * i] for i in range(q)])
                for i in range(q):
                    base = mass if axis == 0 else dst
                    r[i] = base[start + step * i] + r[i]
                if axis == 2:
                    r = z_sum(r, lanes)
                for i in range(q):
                    dst[start + step * i] = r[i]


def kernel(
    nx,
    ny,
    src_ref,
    cond_ref,
    abs_ref,
    out_ref,
    cor_ref,
    wide,
    raw,
    craw,
    perm,
    back,
    cback,
    load,
    inv,
    power,
    w0,
    w1,
    w2,
    b,
    power_2,
    flux,
    mass,
    coarse,
    cflux,
    cmass,
    tmp_a,
    tmp_b,
    send,
    recv,
    line_x_send,
    line_x,
    line_y_send,
    line_y,
    send_sem,
    recv_sem,
    line_send_sem,
    line_x_sem,
    line_y_sem,
):
    px, py, pz = src_ref.shape
    ex, ey, ez = px // QF, py // QF, pz // QF
    subs, lanes = ex * ey, ez
    rows_x = -(-py // 8) * 8
    rows = px * rows_x
    mx, my = lax.axis_index("gx"), lax.axis_index("gy")

    def target(dx, dy):
        return (lax.rem(mx + dx + nx, nx), lax.rem(my + dy + ny, ny))

    greeted = {(o, 0) for o in range(1, nx)} | {(0, o) for o in range(1, ny)}
    greeted |= {(dx % nx, dy % ny) for dx, dy in DIRS}
    greeted = sorted(greeted)
    barrier = pltpu.get_barrier_semaphore()
    for dx, dy in greeted:
        pl.semaphore_signal(barrier, inc=1, device_id=target(dx, dy), device_id_type=MESH)

    sub = lax.broadcasted_iota(jnp.int32, (subs, lanes), 0)

    def any_of(indices):
        mask = None
        for index in indices:
            one = sub == index
            mask = one if mask is None else mask | one
        return mask

    x_group = [(sub >= j * ey) & (sub < (j + 1) * ey) for j in range(ex)]
    y_group = [any_of([e * ey + j for e in range(ex)]) for j in range(ey)]
    at_sub = {}

    def single(index):
        if index not in at_sub:
            at_sub[index] = sub == index
        return at_sub[index]

    def shifted(plane, shift):
        shift = shift % subs
        return plane if shift == 0 else pltpu.roll(plane, shift, 0)

    def layout(d):
        dx, dy = DIRS[d]
        if dy == 0:
            return ex, ey, (0 if dx < 0 else ex - 1), (ex - 1 if dx < 0 else 0)
        if dx == 0:
            return ey, 1, (0 if dy < 0 else ey - 1), (ey - 1 if dy < 0 else 0)
        sx, tx = (0, ex - 1) if dx < 0 else (ex - 1, 0)
        sy, ty = (0, ey - 1) if dy < 0 else (ey - 1, 0)
        return subs, 1, sx * ey + sy, tx * ey + ty

    def group_mask(d, j):
        dx, dy = DIRS[d]
        if dy == 0:
            return x_group[j]
        if dx == 0:
            return y_group[j]
        return single(j)

    def face_planes(d, q):
        dx, dy = DIRS[d]
        xs = range(q) if dx == 0 else [0 if dx < 0 else q - 1]
        ys = range(q) if dy == 0 else [0 if dy < 0 else q - 1]
        return [(x * q + y) * q + z for x in xs for y in ys for z in range(q)]

    def copy_of(stage, d, tiles):
        return pltpu.make_async_remote_copy(
            src_ref=send.at[stage, d, pl.ds(0, tiles)],
            dst_ref=recv.at[stage, d, pl.ds(0, tiles)],
            send_sem=send_sem.at[stage, d],
            recv_sem=recv_sem.at[stage, d],
            device_id=target(*DIRS[d]),
            device_id_type=MESH,
        )

    pending = []

    def start_exchange(stage, fields):
        copies = []
        for d in range(len(DIRS)):
            groups, distance, source, _ = layout(d)
            planes = [ref.at[p] for ref, q in fields for p in face_planes(d, q)]
            tiles = -(-len(planes) // groups)
            for t in range(tiles):
                acc = None
                for j, plane in enumerate(planes[t * groups : (t + 1) * groups]):
                    moved = shifted(plane[...], (j - source) * distance)
                    acc = moved if acc is None else jnp.where(group_mask(d, j), moved, acc)
                send[stage, d, t] = acc
            copy = copy_of(stage, d, tiles)
            copy.start()
            copies.append(copy)
        return copies

    not_first_x, not_last_x = sub >= ey, sub < (ex - 1) * ey
    first_y, last_y = y_group[0], y_group[ey - 1]

    def finish_exchange(stage, fields, copies):
        for copy in copies:
            copy.wait_recv()
        pending.extend(copies)

        def received(d, number):
            groups, distance, _, place = layout(d)
            tile, j = divmod(number, groups)
            return shifted(recv[stage, d, tile], (place - j) * distance)

        offsets = [0] * len(DIRS)
        for ref, q in fields:
            last = q - 1
            plane = lambda x, y, z: (x * q + y) * q + z

            def x_sum(lo, hi, from_low, from_high):
                new_lo = lo + jnp.where(not_first_x, shifted(hi, ey), from_low)
                new_hi = hi + jnp.where(not_last_x, shifted(lo, -ey), from_high)
                return new_lo, new_hi

            for y in range(q):
                for z in range(q):
                    number = y * q + z
                    lo, hi = x_sum(
                        ref[plane(0, y, z)],
                        ref[plane(last, y, z)],
                        received(1, offsets[1] + number),
                        received(0, offsets[0] + number),
                    )
                    ref[plane(0, y, z)] = lo
                    ref[plane(last, y, z)] = hi
            for z in range(q):
                low = [received(3, offsets[3] + x * q + z) for x in range(q)]
                high = [received(2, offsets[2] + x * q + z) for x in range(q)]
                low[0], low[last] = x_sum(
                    low[0], low[last], received(7, offsets[7] + z), received(5, offsets[5] + z)
                )
                high[0], high[last] = x_sum(
                    high[0], high[last], received(6, offsets[6] + z), received(4, offsets[4] + z)
                )
                for x in range(q):
                    lo, hi = ref[plane(x, 0, z)], ref[plane(x, last, z)]
                    ref[plane(x, 0, z)] = lo + jnp.where(first_y, low[x], shifted(hi, 1))
                    ref[plane(x, last, z)] = hi + jnp.where(last_y, high[x], shifted(lo, -1))
            for d in range(len(DIRS)):
                offsets[d] += len(face_planes(d, q))

    def start_line(which, along_x, first, second):
        out, slots, sems = (
            (line_x_send, line_x, line_x_sem) if along_x else (line_y_send, line_y, line_y_sem)
        )
        count = nx if along_x else ny
        out[which, 0:1] = first
        out[which, 1:2] = second
        copies = []
        for o in range(1, count):
            copy = pltpu.make_async_remote_copy(
                src_ref=out.at[which],
                dst_ref=slots.at[which, o],
                send_sem=line_send_sem.at[which, 0 if along_x else 1, o],
                recv_sem=sems.at[which, o],
                device_id=target(o, 0) if along_x else target(0, o),
                device_id_type=MESH,
            )
            copy.start()
            copies.append(copy)
        return copies

    def finish_line(which, along_x, copies):
        out, slots = (line_x_send, line_x) if along_x else (line_y_send, line_y)
        count = nx if along_x else ny
        for copy in copies:
            copy.wait_recv()
        pending.extend(copies)
        total = out[which]
        for o in range(1, count):
            total = total + slots[which, o]
        return total[0:1], total[1:2]

    def inverse_estimate(first, second):
        first = jnp.sum(first, axis=1, keepdims=True)
        second = jnp.sum(second, axis=1, keepdims=True)
        return 1.0 / jnp.sqrt(second / (first + 1e-06))

    def coefficients(inv_est):
        power = inv_est
        out = []
        for c in CHEB:
            out.append(jnp.broadcast_to(c * power, (subs, lanes)))
            power = power * inv_est
        return out

    for k in range(QF):
        row = lax.broadcasted_iota(jnp.int32, (pz, ez), 0)
        col = lax.broadcasted_iota(jnp.int32, (pz, ez), 1)
        perm[:, k * ez : (k + 1) * ez] = jnp.where(row == QF * col + k, 1.0, 0.0).astype(
            jnp.bfloat16
        )

    def transposed_permutation(ref, q):
        for k in range(q):
            row = lax.broadcasted_iota(jnp.int32, (ez, q * ez), 0)
            col = lax.broadcasted_iota(jnp.int32, (ez, q * ez), 1)
            ref[k * ez : (k + 1) * ez, :] = jnp.where(col == q * row + k, 1.0, 0.0).astype(
                jnp.bfloat16
            )

    def split_dot(value, table):
        high = value.astype(jnp.bfloat16)
        rest = value - high.astype(jnp.float32)
        mid = rest.astype(jnp.bfloat16)
        low = (rest - mid.astype(jnp.float32)).astype(jnp.bfloat16)
        dot = functools.partial(jnp.dot, preferred_element_type=jnp.float32)
        return dot(high, table) + (dot(mid, table) + dot(low, table))

    for n, ref in enumerate((src_ref, cond_ref, abs_ref)):
        for x in range(px):
            wide[n * rows + x * rows_x : n * rows + x * rows_x + py, :] = ref[x]
    chunk = rows // 2

    @pl.loop(0, 6)
    def _(c):
        at = pl.multiple_of(c * chunk, 8)
        moved = split_dot(wide[pl.ds(at, chunk), :], perm[...])
        for k in range(QF):
            raw[k, pl.ds(at, chunk), :] = moved[:, k * ez : (k + 1) * ez]

    pick = {0: 0, 2: 1, 4: 2}
    for x in range(QF):
        for y in range(QF):
            for z in range(QF):
                p = (x * QF + y) * QF + z
                weight = float(FINE_W[x] * FINE_W[y] * FINE_W[z])
                on_coarse = x in pick and y in pick and z in pick
                for e in range(ex):
                    at = (e * QF + x) * rows_x + y
                    values = [
                        raw[z, pl.ds(n * rows + at, ey, stride=QF), :] for n in range(3)
                    ]
                    place = slice(e * ey, (e + 1) * ey)
                    load[p, place, :] = weight * values[0]
                    flux[p, place, :] = weight * values[1]
                    mass[p, place, :] = weight * values[2]
                    if on_coarse:
                        i, j, k = pick[x], pick[y], pick[z]
                        cp = (i * QC + j) * QC + k
                        cw = float(COARSE_W[i] * COARSE_W[j] * COARSE_W[k])
                        cflux[cp, place, :] = cw * values[1]
                        cmass[cp, place, :] = cw * values[2]

    cinv, cur, crhs, cw0, cb, cpow, cw1, ccor = [coarse.at[i] for i in range(8)]

    def each(q, body):
        @pl.loop(0, q * q)
        def _(a):
            for i in range(q):
                body(a * q + i)

    def squares(q, values):
        def body(a, acc):
            for i in range(q):
                v = values(a * q + i)
                acc = acc + v * v
            return acc

        total = lax.fori_loop(0, q * q, body, jnp.zeros((subs, lanes), jnp.float32))
        return jnp.sum(total, axis=0, keepdims=True)

    def store(dst, values):
        def body(p):
            dst[p] = values(p)

        return body

    def restrict(field, dst):
        if True:

            @pl.loop(0, QF)
            def _(a):
                for c in range(QF):
                    line = dense(RESTRICT, [field[i * QF * QF + a * QF + c] for i in range(QF)])
                    for i in range(QC):
                        tmp_a[i * QF * QF + a * QF + c] = line[i]

        @pl.loop(0, QC)
        def _(a):
            for c in range(QF):
                line = dense(RESTRICT, [tmp_a[a * QF * QF + i * QF + c] for i in range(QF)])
                for i in range(QC):
                    tmp_b[a * QC * QF + i * QF + c] = line[i]

        @pl.loop(0, QC)
        def _(a):
            for c in range(QC):
                line = dense(RESTRICT, [tmp_b[a * QC * QF + c * QF + i] for i in range(QF)])
                line = z_sum(line, lanes)
                for i in range(QC):
                    dst[a * QC * QC + c * QC + i] = line[i]

    def apply_fine(src, dst):
        local_op(src, dst, flux, mass, FINE_D, lanes)

    def apply_coarse(src, dst):
        local_op(src, dst, cflux, cmass, COARSE_D, lanes)

    @pl.loop(0, QF * QF)
    def _(a):
        line = z_sum([load[a * QF + i] for i in range(QF)], lanes)
        load[a * QF] = line[0]
        load[a * QF + QF - 1] = line[-1]

    pl.semaphore_wait(barrier, len(greeted))
    load_fields = [(load, QF)]
    load_copies = start_exchange(7, load_fields)
    local_diag(inv, flux, mass, FINE_D, lanes)
    local_diag(cinv, cflux, cmass, COARSE_D, lanes)
    fields = [(inv, QF), (cinv, QC)]
    copies = start_exchange(0, fields)
    finish_exchange(7, load_fields, load_copies)

    apply_fine(load, power)
    power_fields = [(power, QF)]
    power_copies = start_exchange(8, power_fields)
    finish_exchange(0, fields, copies)

    def invert(p):
        value = 1.0 / inv[p]
        inv[p] = value
        b[p] = value * load[p]

    each(QF, invert)
    each(QC, store(cinv, lambda p: 1.0 / cinv[p]))
    restrict(load, crhs)
    apply_fine(b, w0)
    fields = [(w0, QF), (crhs, QC)]
    copies = start_exchange(1, fields)

    finish_exchange(8, power_fields, power_copies)
    each(QF, store(power, lambda p: inv[p] * power[p]))
    apply_fine(power, power_2)
    power_fields = [(power_2, QF)]
    power_copies = start_exchange(9, power_fields)
    sum_first = squares(QF, lambda p: power[p])

    finish_exchange(1, fields, copies)
    each(QF, store(b, lambda p: inv[p] * w0[p]))
    apply_coarse(crhs, cpow)
    apply_fine(b, w1)
    fields = [(w1, QF), (cpow, QC)]
    copies = start_exchange(2, fields)
    finish_exchange(9, power_fields, power_copies)
    sum_second = squares(QF, lambda p: inv[p] * power_2[p])
    line = start_line(0, True, sum_first, sum_second)
    transposed_permutation(back, QF)
    transposed_permutation(cback, QC)
    finish_exchange(2, fields, copies)
    each(QF, store(b, lambda p: inv[p] * w1[p]))
    each(QC, store(cpow, lambda p: cinv[p] * cpow[p]))

    apply_fine(b, w2)
    line = start_line(0, False, *finish_line(0, True, line))
    apply_coarse(cpow, cur)
    fields = [(w2, QF), (cur, QC)]
    copies = start_exchange(3, fields)
    csum_first = squares(QC, lambda p: cpow[p])
    scale = coefficients(inverse_estimate(*finish_line(0, False, line)))
    finish_exchange(3, fields, copies)
    csum_second = squares(QC, lambda p: cinv[p] * cur[p])
    each(
        QF,
        store(
            b, lambda p: load[p] - (scale[0] * w0[p] + scale[1] * w1[p] + scale[2] * w2[p])
        ),
    )

    restrict(b, crhs)
    fields = [(crhs, QC)]
    copies = start_exchange(4, fields)
    line = start_line(1, True, csum_first, csum_second)
    each(
        QF,
        store(
            power,
            lambda p: inv[p] * (scale[0] * load[p] + scale[1] * w0[p] + scale[2] * w1[p]),
        ),
    )
    finish_exchange(4, fields, copies)
    each(QC, store(cb, lambda p: cinv[p] * crhs[p]))

    apply_coarse(cb, cw0)
    fields = [(cw0, QC)]
    copies = start_exchange(5, fields)
    line = start_line(1, False, *finish_line(1, True, line))
    finish_exchange(5, fields, copies)
    each(QC, store(cb, lambda p: cinv[p] * cw0[p]))

    apply_coarse(cb, cw1)
    fields = [(cw1, QC)]
    copies = start_exchange(6, fields)
    cscale = coefficients(inverse_estimate(*finish_line(1, False, line)))
    finish_exchange(6, fields, copies)
    each(
        QC,
        store(
            ccor,
            lambda p: cinv[p]
            * (cscale[0] * crhs[p] + cscale[1] * cw0[p] + cscale[2] * cw1[p]),
        ),
    )

    for y in range(QC):
        for z in range(QC):
            line = dense(INTERP, [ccor[i * QC * QC + y * QC + z] for i in range(QC)])
            for i in range(QF):
                tmp_a[(i * QC + y) * QC + z] = line[i]
    for x in range(QF):
        for z in range(QC):
            line = dense(INTERP, [tmp_a[(x * QC + i) * QC + z] for i in range(QC)])
            for i in range(QF):
                tmp_b[(x * QF + i) * QC + z] = line[i]
    for x in range(QF):
        for y in range(QF):
            line = dense(INTERP, [tmp_b[(x * QF + y) * QC + i] for i in range(QC)])
            for z in range(QF):
                value = power[(x * QF + y) * QF + z] + line[z]
                for e in range(ex):
                    at = (e * QF + x) * rows_x + y
                    raw[z, pl.ds(at, ey, stride=QF), :] = value[e * ey : (e + 1) * ey]
    crows_x = cor_ref.shape[1] + (-cor_ref.shape[1]) % 8
    for x in range(QC):
        for y in range(QC):
            for z in range(QC):
                value = ccor[(x * QC + y) * QC + z]
                for e in range(ex):
                    at = (e * QC + x) * crows_x + y
                    craw[z, pl.ds(at, ey, stride=QC), :] = value[e * ey : (e + 1) * ey]

    @pl.loop(0, 2)
    def _(c):
        at = pl.multiple_of(c * chunk, 8)
        packed = jnp.concatenate([raw[k, pl.ds(at, chunk), :] for k in range(QF)], axis=1)
        wide[pl.ds(at, chunk), :] = split_dot(packed, back[...])

    for x in range(px):
        out_ref[x] = wide[x * rows_x : x * rows_x + py, :]
    packed = jnp.concatenate([craw[k] for k in range(QC)], axis=1)
    moved = split_dot(packed, cback[...])
    for x in range(cor_ref.shape[0]):
        cor_ref[x] = moved[x * crows_x : x * crows_x + cor_ref.shape[1], :]
    for copy in pending:
        copy.wait_send()


def on_device(nx, ny, source, conductivity, absorption):
    px, py, pz = source.shape
    ex, ey, ez = px // QF, py // QF, pz // QF
    subs = ex * ey
    rows = px * (-(-py // 8) * 8)
    crows = ex * QC * (-(-ey * QC // 8) * 8)
    tiles = -(-(QF * QF + QC * QC) // min(ex, ey))
    f32, bf16 = jnp.float32, jnp.bfloat16
    dirs = len(DIRS)
    longest = max(nx, ny)
    scratch = [
        pltpu.VMEM((3 * rows, pz), f32),
        pltpu.VMEM((QF, 3 * rows, ez), f32),
        pltpu.VMEM((QC, crows, ez), f32),
        pltpu.VMEM((pz, pz), bf16),
        pltpu.VMEM((pz, pz), bf16),
        pltpu.VMEM((QC * ez, QC * ez), bf16),
        *[pltpu.VMEM((QF**3, subs, ez), f32)] * 8,
        pltpu.VMEM((QF**3, subs, ez), f32),
        pltpu.VMEM((QF**3, subs, ez), f32),
        pltpu.VMEM((8, QC**3, subs, ez), f32),
        pltpu.VMEM((QC**3, subs, ez), f32),
        pltpu.VMEM((QC**3, subs, ez), f32),
        pltpu.VMEM((QF * QF * QC, subs, ez), f32),
        pltpu.VMEM((QF * QF * QC, subs, ez), f32),
        pltpu.VMEM((STAGES, dirs, tiles, subs, ez), f32),
        pltpu.VMEM((STAGES, dirs, tiles, subs, ez), f32),
        pltpu.VMEM((2, 8, ez), f32),
        pltpu.VMEM((2, nx, 8, ez), f32),
        pltpu.VMEM((2, 8, ez), f32),
        pltpu.VMEM((2, ny, 8, ez), f32),
        pltpu.SemaphoreType.DMA((STAGES, dirs)),
        pltpu.SemaphoreType.DMA((STAGES, dirs)),
        pltpu.SemaphoreType.DMA((2, 2, longest)),
        pltpu.SemaphoreType.DMA((2, nx)),
        pltpu.SemaphoreType.DMA((2, ny)),
    ]
    vmem = pl.BlockSpec(memory_space=pltpu.VMEM)
    return pl.pallas_call(
        functools.partial(kernel, nx, ny),
        out_shape=(
            jax.ShapeDtypeStruct(source.shape, f32),
            jax.ShapeDtypeStruct((ex * QC, ey * QC, ez * QC), f32),
        ),
        in_specs=[vmem] * 3,
        out_specs=(vmem, vmem),
        scratch_shapes=scratch,
        compiler_params=pltpu.CompilerParams(
            collective_id=0, has_side_effects=True, vmem_limit_bytes=60 * 1024 * 1024
        ),
    )(source, conductivity, absorption)


def solution(mesh):
    spec = P("gx", "gy", None)
    return jax.shard_map(
        functools.partial(on_device, mesh.shape["gx"], mesh.shape["gy"]),
        mesh=mesh,
        in_specs=(spec,) * 3,
        out_specs=(spec, spec),
        check_vma=False,
    )
```

profile of v0, /device:TPU:0, one launch (start us, length us, event | category | flops | bytes accessed | tf_op | source)
XLA Modules:
  0.0 82.6 jit_solution(16899178969283959669)
XLA Ops:
  0.6 78.8 %shard_map.50 = (f32[20,20,640]{2,1,0:T(8,128)}, f32[12,12,384]{2,1,0:T(8,128)}) custom-call(f32[20,20,640]{2,1,0:T(8,128)} %src_ref.1, f32[20,20,640]{2,1,0:T(8,128)} %cond_ref.1, f32[20,20,640]{2,1,0:T(8,128)} %abs_ref.1), custom_call_target="tpu_custom_call" | custom-call | tf_op jit(solution)/shard_map/pallas_call | solution.py:699
  79.4 0.0 copy-start
  79.5 2.4 %copy.7 = f32[20,20,640]{2,1,0:T(8,128)} copy(f32[20,20,640]{2,1,0:T(8,128)} %get-tuple-element.4) | data formatting | bytes 2048000
  81.9 0.0 copy-done
  81.9 0.7 copy.8
Async XLA Ops:
  79.4 2.5 %copy-start = (f32[12,12,384]{2,1,0:T(8,128)S(1)}, f32[12,12,384]{2,1,0:T(8,128)}, u32[]{:S(2)}) copy-start(f32[12,12,384]{2,1,0:T(8,128)} %get-tuple-element.5) | copy-start | bytes 663556
where the time goes:
time: 82.8 us; the launch traced here: 82.6 us
  Pallas kernels  78.8 us (95%)
  local copies, waits for them, and re-layouts  3.16 us (4%)
    pallas_call x1, Pallas kernels, on_device(): pl.pallas_call(functools.partial(kernel, nx, ny), out_shape=(jax.ShapeDty...  78.8 us
    unnamed x4, local copies, waits for them, and re-layouts  3.16 us

commit v1 on v0

v1 whole, which is shorter than its diff:
```python
import functools
import math

import jax
import jax.numpy as jnp
import numpy as np
from jax import lax
from jax.experimental import pallas as pl
from jax.experimental.pallas import tpu as pltpu
from jax.sharding import PartitionSpec as P

SWEEPS = 3
MESH = pl.DeviceIdType.MESH
DIRS = [(-1, -1), (-1, 1), (1, -1), (1, 1), (0, -1), (0, 1), (-1, 0), (1, 0)]
FINE_STAGES, COARSE_STAGES = 6, 6


def deriv_table(points):
    count = len(points)
    barycentric = np.array(
        [
            1.0 / np.prod([points[j] - points[k] for k in range(count) if k != j])
            for j in range(count)
        ]
    )
    table = np.zeros((count, count))
    for i in range(count):
        for j in range(count):
            if i != j:
                table[i, j] = barycentric[j] / (barycentric[i] * (points[i] - points[j]))
        table[i, i] = -np.sum(table[i])
    return table


ROOT = math.sqrt(3.0 / 7.0)
FINE_POINTS = np.array([-1.0, -ROOT, 0.0, ROOT, 1.0])
FINE_W = np.array([0.1, 49.0 / 90.0, 32.0 / 45.0, 49.0 / 90.0, 0.1])
COARSE_POINTS = np.array([-1.0, 0.0, 1.0])
COARSE_W = np.array([1.0 / 3.0, 4.0 / 3.0, 1.0 / 3.0])
FINE_D = deriv_table(FINE_POINTS)
COARSE_D = deriv_table(COARSE_POINTS)
INTERP = np.stack(
    [
        FINE_POINTS * (FINE_POINTS - 1.0) / 2.0,
        1.0 - FINE_POINTS**2,
        FINE_POINTS * (FINE_POINTS + 1.0) / 2.0,
    ],
    1,
)
RESTRICT = INTERP.T * np.array([0.5, 1.0, 1.0, 1.0, 0.5])[None, :]
TRANSFER = INTERP.T
QF, QC = 5, 3


def chebyshev_coefficients():
    theta, delta, sigma, rho = 0.75, 0.45, 5.0 / 3.0, 0.6
    x = np.zeros(SWEEPS + 1)
    r = np.zeros(SWEEPS + 1)
    r[0] = 1.0
    d = r / theta
    for sweep in range(SWEEPS):
        x = x + d
        r = r - np.concatenate([[0.0], d[:-1]])
        if sweep + 1 < SWEEPS:
            rho_next = 1.0 / (2.0 * sigma - rho)
            d = rho_next * rho * d + 2.0 * rho_next / delta * r
            rho = rho_next
    return [float(v) for v in x[:SWEEPS]]


CHEB = chebyshev_coefficients()


def antisym(table, u):
    n = len(u)
    half = n // 2
    even = [u[j] + u[n - 1 - j] for j in range(half)]
    odd = [u[j] - u[n - 1 - j] for j in range(half)]
    out = [None] * n
    for i in range(half):
        p = float(table[i, half]) * u[half]
        q = None
        for j in range(half):
            s = (table[i, j] + table[i, n - 1 - j]) / 2
            t = (table[i, j] - table[i, n - 1 - j]) / 2
            p = p + float(s) * even[j]
            q = float(t) * odd[j] if q is None else q + float(t) * odd[j]
        out[i] = q + p
        out[n - 1 - i] = q - p
    mid = None
    for j in range(half):
        term = float(table[half, j]) * odd[j]
        mid = term if mid is None else mid + term
    out[half] = mid
    return out


def dense(table, u):
    out = []
    for i in range(table.shape[0]):
        acc = None
        for j in range(table.shape[1]):
            c = float(table[i, j])
            if abs(c) < 1e-14:
                continue
            term = u[j] if c == 1.0 else c * u[j]
            acc = term if acc is None else acc + term
        out.append(acc)
    return out


def plane_starts(q, axis, a, b):
    strides = (q * q, q, 1)
    other = [s for k, s in enumerate(strides) if k != axis]
    return a * other[0] + b * other[1], strides[axis]


def z_sum(line, lanes):
    lo, hi = line[0], line[-1]
    line[-1] = hi + pltpu.roll(lo, lanes - 1, 1)
    line[0] = lo + pltpu.roll(hi, 1, 1)
    return line


def local_op(src, dst, flux, mass, table, lanes):
    q = table.shape[0]

    def lines(axis, a):
        def read(b):
            start, step = plane_starts(q, axis, a, b)
            u = [src[start + step * i] for i in range(q)]
            base = None if axis == 0 else [dst[start + step * i] for i in range(q)]
            return u, base

        ahead = read(0)
        for b in range(q):
            u, base = ahead
            if b + 1 < q:
                ahead = read(b + 1)
            start, step = plane_starts(q, axis, a, b)
            g = antisym(table, u)
            g = [flux[start + step * i] * g[i] for i in range(q)]
            r = antisym(table.T, g)
            for i in range(q):
                r[i] = (mass[start + step * i] * u[i] if base is None else base[i]) + r[i]
            if axis == 2:
                r = z_sum(r, lanes)
            for i in range(q):
                dst[start + step * i] = r[i]

    for axis in range(2):

        @pl.loop(0, q)
        def _(a, axis=axis):
            lines(axis, a)

    for a in range(q):
        lines(2, a)


def local_diag(dst, flux, mass, table, lanes):
    q = table.shape[0]
    square = (table * table).T

    def lines(axis, a):
        for b in range(q):
            start, step = plane_starts(q, axis, a, b)
            r = dense(square, [flux[start + step * i] for i in range(q)])
            for i in range(q):
                base = mass if axis == 0 else dst
                r[i] = base[start + step * i] + r[i]
            if axis == 2:
                r = z_sum(r, lanes)
            for i in range(q):
                dst[start + step * i] = r[i]

    for axis in range(2):

        @pl.loop(0, q)
        def _(a, axis=axis):
            lines(axis, a)

    for a in range(q):
        lines(2, a)


class Lanes:
    def __init__(self, q, rows, ez):
        self.q, self.rows, self.ez = q, rows, ez
        lane = lax.broadcasted_iota(jnp.int32, (rows, ez), 1)
        self.turn = ez % q
        self.back = pow(self.turn, -1, q)
        unit = pow(q, -1, ez)
        self.pick = [lax.rem(lane * q + k, ez) for k in range(q)]
        self.place = [lax.rem((lane + (ez - k)) * unit, ez) for k in range(q)]
        s = lax.rem(lane, q)
        self.out_steps = self.bits(lax.rem(s * (q - self.back), q))
        self.in_steps = self.bits(lax.rem(s * self.back, q))

    def bits(self, amount):
        steps, step = [], 1
        while step < self.q:
            steps.append((step, lax.rem(lax.div(amount, step), 2) == 1))
            step *= 2
        return steps

    def select(self, blocks, steps):
        for step, mask in steps:
            blocks = [
                jnp.where(mask, blocks[(v + step) % self.q], blocks[v]) for v in range(self.q)
            ]
        return blocks

    def split(self, blocks):
        mixed = self.select(blocks, self.out_steps)
        return [
            jnp.take_along_axis(mixed[self.back * k % self.q], self.pick[k], axis=1)
            for k in range(self.q)
        ]

    def merge(self, planes):
        mixed = []
        for j in range(self.q):
            k = self.turn * j % self.q
            mixed.append(jnp.take_along_axis(planes[k], self.place[k], axis=1))
        return self.select(mixed, self.in_steps)


def kernel(
    nx,
    ny,
    src_hbm,
    cond_hbm,
    abs_hbm,
    out_hbm,
    cor_hbm,
    stored,
    result,
    cresult,
    load,
    inv,
    power,
    power_2,
    b0,
    b1,
    b2,
    flux,
    mass,
    smooth,
    coarse,
    tmp_a,
    tmp_b,
    fine_send,
    fine_recv,
    coarse_send,
    coarse_recv,
    line_x_send,
    line_x,
    line_y_send,
    line_y,
    in_sem,
    out_sem,
    cor_sem,
    fine_sems,
    coarse_sems,
    line_send_sem,
    line_x_sem,
    line_y_sem,
):
    px, py, pz = src_hbm.shape
    ex, ey, ez = px // QF, py // QF, pz // QF
    subs, lanes = ex * ey, ez
    tile = 8
    mx, my = lax.axis_index("gx"), lax.axis_index("gy")

    def target(dx, dy):
        return (lax.rem(mx + dx + nx, nx), lax.rem(my + dy + ny, ny))

    greeted = {(o, 0) for o in range(1, nx)} | {(0, o) for o in range(1, ny)}
    greeted |= {(dx % nx, dy % ny) for dx, dy in DIRS}
    greeted = sorted(greeted)
    barrier = pltpu.get_barrier_semaphore()
    for dx, dy in greeted:
        pl.semaphore_signal(barrier, inc=1, device_id=target(dx, dy), device_id_type=MESH)

    arriving = []
    for n, ref in enumerate((src_hbm, cond_hbm, abs_hbm)):
        for v in range(QF):
            copy = pltpu.make_async_copy(
                ref.at[:, :, v * ez : (v + 1) * ez], stored.at[n, v], in_sem.at[n, v]
            )
            copy.start()
            arriving.append(copy)

    sub = lax.broadcasted_iota(jnp.int32, (subs, lanes), 0)
    row_y = lax.rem(sub, ey)
    first_x, last_x = sub < ey, sub >= (ex - 1) * ey
    first_y, last_y = row_y == 0, row_y == ey - 1

    def shifted(plane, shift):
        return pltpu.roll(plane, shift % subs, 0)

    def local_sum(ref, q, zs):
        last = q - 1
        for z in zs:
            for y in range(q):
                p, r = y * q + z, (last * q + y) * q + z
                lo, hi = ref[p], ref[r]
                ref[p] = jnp.where(first_x, lo, lo + shifted(hi, ey))
                ref[r] = jnp.where(last_x, hi, hi + shifted(lo, -ey))
            for x in range(q):
                p, r = x * q * q + z, (x * q + last) * q + z
                lo, hi = ref[p], ref[r]
                ref[p] = jnp.where(first_y, lo, lo + shifted(hi, 1))
                ref[r] = jnp.where(last_y, hi, hi + shifted(lo, -1))

    def edge(dx, dy, q):
        xs = range(q) if dx == 0 else [0 if dx < 0 else q - 1]
        ys = range(q) if dy == 0 else [0 if dy < 0 else q - 1]
        planes = [(x * q + y) * q + z for x in xs for y in ys for z in range(q - 1)]
        e, f = (0 if dx < 0 else ex - 1), (0 if dy < 0 else ey - 1)
        if dy == 0:
            return planes, ey, slice(e * ey, (e + 1) * ey)
        if dx == 0:
            return planes, ex, pl.ds(f, ex, stride=ey)
        return planes, 1, slice(e * ey + f, e * ey + f + 1)

    def whole_rows(count):
        return -(-count // tile) * tile

    pending = []

    def start_exchange(level, stage, fields):
        send, recv, sems = level
        copies = []
        for d, (dx, dy) in enumerate(DIRS):
            at = 0
            for ref, q in fields:
                planes, count, rows = edge(dx, dy, q)
                for p in planes:
                    send[stage, d, at : at + count, :] = ref[p, rows, :]
                    at += count
            total = whole_rows(at)
            copy = pltpu.make_async_remote_copy(
                src_ref=send.at[stage, d, pl.ds(0, total)],
                dst_ref=recv.at[stage, d, pl.ds(0, total)],
                send_sem=sems.at[0, stage, d],
                recv_sem=sems.at[1, stage, d],
                device_id=target(dx, dy),
                device_id_type=MESH,
            )
            copy.start()
            copies.append(copy)
        return copies

    def finish_exchange(level, stage, fields, copies, finals):
        _, recv, _ = level
        for d in reversed(range(len(DIRS))):
            dx, dy = DIRS[d]
            copies[d].wait_recv()
            at = 0
            for ref, q in fields:
                planes, count, rows = edge(-dx, -dy, q)
                for p in planes:
                    ref[p, rows, :] = ref[p, rows, :] + recv[stage, d, at : at + count, :]
                    at += count
        pending.extend(copies)
        for (ref, q), final in zip(fields, finals):
            for x in range(q):
                for y in range(q):
                    if x in (0, q - 1) or y in (0, q - 1):
                        p = (x * q + y) * q
                        for z in range(q - 1):
                            value = final(p + z, ref[p + z])
                            ref[p + z] = value
                            if z == 0:
                                ref[p + q - 1] = pltpu.roll(value, lanes - 1, 1)

    def interior(ref, q, final):
        for x in range(1, q - 1):
            for y in range(1, q - 1):
                for z in range(q):
                    p = (x * q + y) * q + z
                    ref[p] = final(p, ref[p])

    fine = (fine_send, fine_recv, fine_sems)
    rough = (coarse_send, coarse_recv, coarse_sems)

    def start_line(which, along_x, first, second):
        out, slots, sems = (
            (line_x_send, line_x, line_x_sem) if along_x else (line_y_send, line_y, line_y_sem)
        )
        count = nx if along_x else ny
        out[which, 0:1] = first
        out[which, 1:2] = second
        copies = []
        for o in range(1, count):
            copy = pltpu.make_async_remote_copy(
                src_ref=out.at[which],
                dst_ref=slots.at[which, o],
                send_sem=line_send_sem.at[which, 0 if along_x else 1, o],
                recv_sem=sems.at[which, o],
                device_id=target(o, 0) if along_x else target(0, o),
                device_id_type=MESH,
            )
            copy.start()
            copies.append(copy)
        return copies

    def finish_line(which, along_x, copies):
        out, slots = (line_x_send, line_x) if along_x else (line_y_send, line_y)
        count = nx if along_x else ny
        for copy in copies:
            copy.wait_recv()
        pending.extend(copies)
        total = out[which]
        for o in range(1, count):
            total = total + slots[which, o]
        return total[0:1], total[1:2]

    def inverse_estimate(first, second):
        first = jnp.sum(first, axis=1, keepdims=True)
        second = jnp.sum(second, axis=1, keepdims=True)
        return 1.0 / jnp.sqrt(second / (first + 1e-06))

    def coefficients(inv_est):
        power = inv_est
        out = []
        for c in CHEB:
            out.append(jnp.broadcast_to(c * power, (subs, lanes)))
            power = power * inv_est
        return out

    net = Lanes(QF, tile, ez)
    group = tile // ey

    def read_planes(n, x, y):
        tiles = []
        for h in range(subs // tile):
            blocks = []
            for v in range(QF):
                parts = [
                    stored[n, v, (h * group + e) * QF + x, pl.ds(y, ey, stride=QF), :]
                    for e in range(group)
                ]
                blocks.append(jnp.concatenate(parts, axis=0))
            tiles.append(net.split(blocks))
        return tiles

    (
        cflux,
        cmass,
        cinv,
        rload,
        cpow,
        cpow_2,
        rw0,
        rw1,
        rw2,
        crhs,
        cb,
        cw0,
        cw1,
        ccor,
    ) = [coarse.at[i] for i in range(14)]

    for copy in arriving[:QF]:
        copy.wait()
    for x in range(QF):
        for y in range(QF):
            weight = [float(FINE_W[x] * FINE_W[y] * w) for w in FINE_W]
            for h, values in enumerate(read_planes(0, x, y)):
                line = z_sum([w * v for w, v in zip(weight, values)], lanes)
                for z in range(QF):
                    load[(x * QF + y) * QF + z, h * tile : (h + 1) * tile, :] = line[z]
    local_sum(load, QF, range(QF - 1))

    def each(q, body):
        @pl.loop(0, q * q)
        def _(a):
            for i in range(q):
                body(a * q + i)

    def squares(q, values):
        def body(a, acc):
            for i in range(q):
                v = values(a * q + i)
                acc = acc + v * v
            return acc

        total = lax.fori_loop(0, q * q, body, jnp.zeros((subs, lanes), jnp.float32))
        return jnp.sum(total, axis=0, keepdims=True)

    def store(dst, values):
        def body(p):
            dst[p] = values(p)

        return body

    def half_unless(mask):
        return jnp.where(mask, 1.0, 0.5)

    def weighted(line, ends):
        if ends is None:
            return line
        return [half_unless(ends[0]) * line[0]] + line[1:-1] + [half_unless(ends[1]) * line[-1]]

    def restrict(field, dst, summed):
        ends_x = (first_x, last_x) if summed else None
        ends_y = (first_y, last_y) if summed else None

        @pl.loop(0, QF)
        def _(a):
            for c in range(QF):
                line = [field[i * QF * QF + a * QF + c] for i in range(QF)]
                line = dense(TRANSFER, weighted(line, ends_x))
                for i in range(QC):
                    tmp_a[i * QF * QF + a * QF + c] = line[i]

        for a in range(QC):
            for c in range(QF):
                line = [tmp_a[a * QF * QF + i * QF + c] for i in range(QF)]
                line = dense(TRANSFER, weighted(line, ends_y))
                for i in range(QC):
                    tmp_b[a * QC * QF + i * QF + c] = line[i]

        for a in range(QC):
            for c in range(QC):
                line = dense(RESTRICT, [tmp_b[a * QC * QF + c * QF + i] for i in range(QF)])
                line = z_sum(line, lanes)
                for i in range(QC):
                    dst[a * QC * QC + c * QC + i] = line[i]

    def apply_fine(src, dst):
        local_op(src, dst, flux, mass, FINE_D, lanes)

    def apply_coarse(src, dst):
        local_op(src, dst, cflux, cmass, COARSE_D, lanes)

    keep = lambda p, v: v
    invert = lambda p, v: 1.0 / v
    scaled = lambda p, v: inv[p] * v
    cscaled = lambda p, v: cinv[p] * v
    inner_f, inner_c = range(QF - 1), range(QC - 1)

    pl.semaphore_wait(barrier, len(greeted))
    f_load = start_exchange(fine, 0, [(load, QF)])

    pick = {0: 0, 2: 1, 4: 2}
    for n, full, part in ((1, flux, cflux), (2, mass, cmass)):
        for copy in arriving[n * QF : (n + 1) * QF]:
            copy.wait()
        for x in range(QF):
            for y in range(QF):
                for h, values in enumerate(read_planes(n, x, y)):
                    place = slice(h * tile, (h + 1) * tile)
                    for z in range(QF):
                        weight = float(FINE_W[x] * FINE_W[y] * FINE_W[z])
                        full[(x * QF + y) * QF + z, place, :] = weight * values[z]
                        if x in pick and y in pick and z in pick:
                            i, j, k = pick[x], pick[y], pick[z]
                            weight = float(COARSE_W[i] * COARSE_W[j] * COARSE_W[k])
                            part[(i * QC + j) * QC + k, place, :] = weight * values[z]

    local_diag(inv, flux, mass, FINE_D, lanes)
    local_sum(inv, QF, inner_f)
    f_diag = start_exchange(fine, 1, [(inv, QF)])

    local_sum(load, QF, [QF - 1])
    restrict(load, rload, True)
    local_sum(rload, QC, inner_c)
    local_diag(cinv, cflux, cmass, COARSE_D, lanes)
    local_sum(cinv, QC, inner_c)
    c_0 = start_exchange(rough, 0, [(cinv, QC), (rload, QC)])
    interior(inv, QF, invert)

    finish_exchange(fine, 0, [(load, QF)], f_load, [keep])
    apply_fine(load, power)
    local_sum(power, QF, inner_f)
    f_power = start_exchange(fine, 2, [(power, QF)])
    interior(power, QF, scaled)

    finish_exchange(fine, 1, [(inv, QF)], f_diag, [invert])
    each(QF, store(b0, lambda p: inv[p] * load[p]))
    apply_fine(b0, b1)
    local_sum(b1, QF, inner_f)
    f_w0 = start_exchange(fine, 3, [(b1, QF)])

    local_sum(b1, QF, [QF - 1])
    restrict(b1, rw0, True)
    local_sum(rw0, QC, inner_c)
    interior(b1, QF, scaled)
    interior(cinv, QC, invert)
    finish_exchange(rough, 0, [(cinv, QC), (rload, QC)], c_0, [invert, keep])
    apply_coarse(rload, cpow)
    local_sum(cpow, QC, inner_c)
    c_1 = start_exchange(rough, 1, [(cpow, QC), (rw0, QC)])
    interior(cpow, QC, cscaled)

    finish_exchange(fine, 2, [(power, QF)], f_power, [scaled])
    apply_fine(power, power_2)
    local_sum(power_2, QF, inner_f)
    f_power_2 = start_exchange(fine, 4, [(power_2, QF)])
    interior(power_2, QF, scaled)

    finish_exchange(fine, 3, [(b1, QF)], f_w0, [scaled])
    apply_fine(b1, b2)
    local_sum(b2, QF, inner_f)
    f_w1 = start_exchange(fine, 5, [(b2, QF)])

    local_sum(b2, QF, [QF - 1])
    restrict(b2, rw1, True)
    local_sum(rw1, QC, inner_c)
    interior(b2, QF, scaled)
    finish_exchange(rough, 1, [(cpow, QC), (rw0, QC)], c_1, [cscaled, keep])
    apply_coarse(cpow, cpow_2)
    local_sum(cpow_2, QC, inner_c)
    c_2 = start_exchange(rough, 2, [(cpow_2, QC), (rw1, QC)])
    interior(cpow_2, QC, cscaled)
    sum_first = squares(QF, lambda p: power[p])

    finish_exchange(fine, 4, [(power_2, QF)], f_power_2, [scaled])
    sum_second = squares(QF, lambda p: power_2[p])
    line = start_line(0, True, sum_first, sum_second)

    finish_exchange(fine, 5, [(b2, QF)], f_w1, [scaled])
    apply_fine(b2, power)
    restrict(power, rw2, False)
    local_sum(rw2, QC, inner_c)
    c_3 = start_exchange(rough, 3, [(rw2, QC)])

    line = start_line(0, False, *finish_line(0, True, line))
    finish_exchange(rough, 2, [(cpow_2, QC), (rw1, QC)], c_2, [cscaled, keep])
    csum_first = squares(QC, lambda p: cpow[p])
    csum_second = squares(QC, lambda p: cpow_2[p])
    cline = start_line(1, True, csum_first, csum_second)
    scale = coefficients(inverse_estimate(*finish_line(0, False, line)))
    each(
        QF,
        store(smooth, lambda p: scale[0] * b0[p] + scale[1] * b1[p] + scale[2] * b2[p]),
    )
    each(QC, store(crhs, lambda p: rload[p] - (scale[0] * rw0[p] + scale[1] * rw1[p])))

    finish_exchange(rough, 3, [(rw2, QC)], c_3, [keep])
    each(QC, store(crhs, lambda p: crhs[p] - scale[2] * rw2[p]))
    each(QC, store(cb, lambda p: cinv[p] * crhs[p]))
    apply_coarse(cb, cw0)
    local_sum(cw0, QC, inner_c)
    c_4 = start_exchange(rough, 4, [(cw0, QC)])
    interior(cw0, QC, cscaled)
    cline = start_line(1, False, *finish_line(1, True, cline))

    finish_exchange(rough, 4, [(cw0, QC)], c_4, [cscaled])
    apply_coarse(cw0, cw1)
    local_sum(cw1, QC, inner_c)
    c_5 = start_exchange(rough, 5, [(cw1, QC)])
    interior(cw1, QC, cscaled)
    cscale = coefficients(inverse_estimate(*finish_line(1, False, cline)))
    each(QC, store(ccor, lambda p: cscale[0] * cb[p] + cscale[1] * cw0[p]))

    finish_exchange(rough, 5, [(cw1, QC)], c_5, [cscaled])
    each(QC, store(ccor, lambda p: ccor[p] + cscale[2] * cw1[p]))

    def write_planes(dst, q, x, y, values, lane_net):
        for h in range(subs // tile):
            rows = slice(h * tile, (h + 1) * tile)
            for v, block in enumerate(lane_net.merge([value[rows] for value in values])):
                for e in range(group):
                    part = block[e * ey : (e + 1) * ey]
                    dst[v, x, h * group + e, pl.ds(y, ey, stride=q), :] = part

    leaving = []
    cnet = Lanes(QC, tile, ez)
    for x in range(QC):
        for y in range(QC):
            values = [ccor[(x * QC + y) * QC + z] for z in range(QC)]
            write_planes(cresult, QC, x, y, values, cnet)
        for v in range(QC):
            copy = pltpu.make_async_copy(
                cresult.at[v, x], cor_hbm.at[:, x, :, v * ez : (v + 1) * ez], cor_sem.at[v, x]
            )
            copy.start()
            leaving.append(copy)
    for y in range(QC):
        for z in range(QC):
            line = dense(INTERP, [ccor[i * QC * QC + y * QC + z] for i in range(QC)])
            for i in range(QF):
                tmp_a[(i * QC + y) * QC + z] = line[i]
    for x in range(QF):
        for z in range(QC):
            line = dense(INTERP, [tmp_a[(x * QC + i) * QC + z] for i in range(QC)])
            for i in range(QF):
                tmp_b[(x * QF + i) * QC + z] = line[i]
        for y in range(QF):
            line = dense(INTERP, [tmp_b[(x * QF + y) * QC + i] for i in range(QC)])
            values = [smooth[(x * QF + y) * QF + z] + line[z] for z in range(QF)]
            write_planes(result, QF, x, y, values, net)
        for v in range(QF):
            copy = pltpu.make_async_copy(
                result.at[v, x], out_hbm.at[:, x, :, v * ez : (v + 1) * ez], out_sem.at[v, x]
            )
            copy.start()
            leaving.append(copy)
    for copy in pending:
        copy.wait_send()
    for copy in leaving:
        copy.wait()


def on_device(nx, ny, source, conductivity, absorption):
    px, py, pz = source.shape
    ex, ey, ez = px // QF, py // QF, pz // QF
    subs = ex * ey
    face = max(ex, ey)
    f32 = jnp.float32
    dirs = len(DIRS)
    longest = max(nx, ny)
    fine_rows = -(-QF * (QF - 1) * face // 8) * 8
    coarse_rows = -(-2 * QC * (QC - 1) * face // 8) * 8
    scratch = [
        pltpu.VMEM((3, QF, px, py, ez), f32),
        pltpu.VMEM((QF, QF, ex, py, ez), f32),
        pltpu.VMEM((QC, QC, ex, ey * QC, ez), f32),
        *[pltpu.VMEM((QF**3, subs, ez), f32)] * 10,
        pltpu.VMEM((14, QC**3, subs, ez), f32),
        pltpu.VMEM((QF * QF * QC, subs, ez), f32),
        pltpu.VMEM((QF * QF * QC, subs, ez), f32),
        *[pltpu.VMEM((FINE_STAGES, dirs, fine_rows, ez), f32)] * 2,
        *[pltpu.VMEM((COARSE_STAGES, dirs, coarse_rows, ez), f32)] * 2,
        pltpu.VMEM((2, 8, ez), f32),
        pltpu.VMEM((2, nx, 8, ez), f32),
        pltpu.VMEM((2, 8, ez), f32),
        pltpu.VMEM((2, ny, 8, ez), f32),
        pltpu.SemaphoreType.DMA((3, QF)),
        pltpu.SemaphoreType.DMA((QF, QF)),
        pltpu.SemaphoreType.DMA((QC, QC)),
        pltpu.SemaphoreType.DMA((2, FINE_STAGES, dirs)),
        pltpu.SemaphoreType.DMA((2, COARSE_STAGES, dirs)),
        pltpu.SemaphoreType.DMA((2, 2, longest)),
        pltpu.SemaphoreType.DMA((2, nx)),
        pltpu.SemaphoreType.DMA((2, ny)),
    ]
    anywhere = pl.BlockSpec(memory_space=pl.ANY)
    out, cor = pl.pallas_call(
        functools.partial(kernel, nx, ny),
        out_shape=(
            jax.ShapeDtypeStruct((ex, QF, py, pz), f32),
            jax.ShapeDtypeStruct((ex, QC, ey * QC, ez * QC), f32),
        ),
        in_specs=[anywhere] * 3,
        out_specs=(anywhere, anywhere),
        scratch_shapes=scratch,
        compiler_params=pltpu.CompilerParams(
            collective_id=0, has_side_effects=True, vmem_limit_bytes=40 * 1024 * 1024
        ),
    )(source, conductivity, absorption)
    return out.reshape(source.shape), cor.reshape(ex * QC, ey * QC, ez * QC)


def solution(mesh):
    spec = P("gx", "gy", None)
    return jax.shard_map(
        functools.partial(on_device, mesh.shape["gx"], mesh.shape["gy"]),
        mesh=mesh,
        in_specs=(spec,) * 3,
        out_specs=(spec, spec),
        check_vma=False,
    )
```

time: 82.8 us -> 52.9 us (0.64)
  Pallas kernels: 78.8 us -> 46.4 us
  local copies, waits for them, and re-layouts: 3.16 us -> 5.6 us
    pallas_call x1, Pallas kernels: 78.8 us -> 46.4 us  [on_device(): pl.pallas_call(functools.partial(kernel, nx, ny), out_shape=(jax.ShapeDty...]
    unnamed x4 -> x8, local copies, waits for them, and re-layouts: 3.16 us -> 5.6 us
where the time goes in v1:
time: 52.9 us; the launch traced here: 52.7 us
  Pallas kernels  46.4 us (88%)
  local copies, waits for them, and re-layouts  5.6 us (11%)
  between operations  0.65 us (1%)
    pallas_call x1, Pallas kernels, on_device(): pl.pallas_call(functools.partial(kernel, nx, ny), out_shape=(jax.ShapeDty...  46.4 us
    unnamed x8, local copies, waits for them, and re-layouts  5.6 us

profile of v1, /device:TPU:0, one launch (start us, length us, event | category | flops | bytes accessed | tf_op | source)
XLA Modules:
  0.0 52.7 jit_solution(10022543523239198119)
XLA Ops:
  0.6 0.0 copy-start
  0.6 1.3 %copy-done = f32[20,20,640]{2,1,0:T(8,128)S(1)} copy-done((f32[20,20,640]{2,1,0:T(8,128)S(1)}, f32[20,20,640]{2,1,0:T(8,128)}, u32[]{:S(2)}) %copy-start) | copy-done | bytes 1024024
  1.9 0.0 copy-start.1
  1.9 1.3 %copy-done.1 = f32[20,20,640]{2,1,0:T(8,128)S(1)} copy-done((f32[20,20,640]{2,1,0:T(8,128)S(1)}, f32[20,20,640]{2,1,0:T(8,128)}, u32[]{:S(2)}) %copy-start.1) | copy-done | bytes 1024024
  3.2 0.0 copy-start.2
  3.2 1.3 %copy-done.2 = f32[20,20,640]{2,1,0:T(8,128)S(1)} copy-done((f32[20,20,640]{2,1,0:T(8,128)S(1)}, f32[20,20,640]{2,1,0:T(8,128)}, u32[]{:S(2)}) %copy-start.2) | copy-done | bytes 1024024
  4.5 46.4 %shard_map.50 = (f32[4,5,20,640]{3,2,1,0:T(8,128)S(1)}, f32[4,3,12,384]{3,2,1,0:T(8,128)S(1)}) custom-call(f32[20,20,640]{2,1,0:T(8,128)S(1)} %copy-done, f32[20,20,640]{2,1,0:T(8,128)S(1)} %copy-done.1, f32[20,20,640]{2,1,0:T(8,128)S(1)} %copy-done.2), custom_call_target="tpu_custom_call" | custom-call | tf_op jit(solution)/shard_map/pallas_call | solution.py:744
  50.9 1.0 %copy.7 = f32[20,20,640]{2,1,0:T(8,128)} copy(f32[20,20,640]{2,1,0:T(8,128)S(1)} %bitcast.2) | data formatting | bytes 2048000
  52.0 0.7 %copy.8 = f32[12,12,384]{2,1,0:T(8,128)} copy(f32[12,12,384]{2,1,0:T(8,128)S(1)} %bitcast.3) | data formatting | bytes 442368
Async XLA Ops:
  0.6 1.3 %copy-start = (f32[20,20,640]{2,1,0:T(8,128)S(1)}, f32[20,20,640]{2,1,0:T(8,128)}, u32[]{:S(2)}) copy-start(f32[20,20,640]{2,1,0:T(8,128)} %src_hbm.1) | copy-start | bytes 3072004
  1.9 1.3 %copy-start.1 = (f32[20,20,640]{2,1,0:T(8,128)S(1)}, f32[20,20,640]{2,1,0:T(8,128)}, u32[]{:S(2)}) copy-start(f32[20,20,640]{2,1,0:T(8,128)} %cond_hbm.1) | copy-start | bytes 3072004
  3.2 1.3 %copy-start.2 = (f32[20,20,640]{2,1,0:T(8,128)S(1)}, f32[20,20,640]{2,1,0:T(8,128)}, u32[]{:S(2)}) copy-start(f32[20,20,640]{2,1,0:T(8,128)} %abs_hbm.1) | copy-start | bytes 3072004

commit v2 on v1

--- a/solution.py
+++ b/solution.py
@@ -186,7 +186,7 @@
 
 class Lanes:
     def __init__(self, q, rows, ez):
-        self.q, self.rows, self.ez = q, rows, ez
+        self.q = q
         lane = lax.broadcasted_iota(jnp.int32, (rows, ez), 1)
         self.turn = ez % q
         self.back = pow(self.turn, -1, q)
@@ -194,10 +194,11 @@
         self.pick = [lax.rem(lane * q + k, ez) for k in range(q)]
         self.place = [lax.rem((lane + (ez - k)) * unit, ez) for k in range(q)]
         s = lax.rem(lane, q)
-        self.out_steps = self.bits(lax.rem(s * (q - self.back), q))
-        self.in_steps = self.bits(lax.rem(s * self.back, q))
-
-    def bits(self, amount):
+        self.out_steps = self.bits(s, q - self.back)
+        self.in_steps = self.bits(s, self.back)
+
+    def bits(self, s, by):
+        amount = lax.rem(s * by, self.q)
         steps, step = [], 1
         while step < self.q:
             steps.append((step, lax.rem(lax.div(amount, step), 2) == 1))
@@ -211,19 +212,12 @@
             ]
         return blocks
 
-    def split(self, blocks):
+    def mix(self, blocks):
         mixed = self.select(blocks, self.out_steps)
-        return [
-            jnp.take_along_axis(mixed[self.back * k % self.q], self.pick[k], axis=1)
-            for k in range(self.q)
-        ]
-
-    def merge(self, planes):
-        mixed = []
-        for j in range(self.q):
-            k = self.turn * j % self.q
-            mixed.append(jnp.take_along_axis(planes[k], self.place[k], axis=1))
-        return self.select(mixed, self.in_steps)
+        return [mixed[self.back * k % self.q] for k in range(self.q)]
+
+    def unmix(self, placed):
+        return self.select([placed[self.turn * j % self.q] for j in range(self.q)], self.in_steps)
 
 
 def kernel(
@@ -434,18 +428,26 @@
     net = Lanes(QF, tile, ez)
     group = tile // ey
 
-    def read_planes(n, x, y):
-        tiles = []
-        for h in range(subs // tile):
-            blocks = []
-            for v in range(QF):
-                parts = [
-                    stored[n, v, (h * group + e) * QF + x, pl.ds(y, ey, stride=QF), :]
-                    for e in range(group)
-                ]
-                blocks.append(jnp.concatenate(parts, axis=0))
-            tiles.append(net.split(blocks))
-        return tiles
+    def permuted(plane, index):
+        tiles = [
+            jnp.take_along_axis(plane[h * tile : (h + 1) * tile], index, axis=1)
+            for h in range(subs // tile)
+        ]
+        return jnp.concatenate(tiles, axis=0)
+
+    def read_planes(n, dst):
+        for x in range(QF):
+            for y in range(QF):
+                for h in range(subs // tile):
+                    blocks = []
+                    for v in range(QF):
+                        parts = [
+                            stored[n, v, (h * group + e) * QF + x, pl.ds(y, ey, stride=QF), :]
+                            for e in range(group)
+                        ]
+                        blocks.append(jnp.concatenate(parts, axis=0))
+                    for z, block in enumerate(net.mix(blocks)):
+                        dst[(x * QF + y) * QF + z, h * tile : (h + 1) * tile, :] = block
 
     (
         cflux,
@@ -466,13 +468,16 @@
 
     for copy in arriving[:QF]:
         copy.wait()
-    for x in range(QF):
-        for y in range(QF):
-            weight = [float(FINE_W[x] * FINE_W[y] * w) for w in FINE_W]
-            for h, values in enumerate(read_planes(0, x, y)):
-                line = z_sum([w * v for w, v in zip(weight, values)], lanes)
-                for z in range(QF):
-                    load[(x * QF + y) * QF + z, h * tile : (h + 1) * tile, :] = line[z]
+    read_planes(0, load)
+    for z in range(QF):
+        for x in range(QF):
+            for y in range(QF):
+                p = (x * QF + y) * QF + z
+                load[p] = float(FINE_W[x] * FINE_W[y] * FINE_W[z]) * permuted(load[p], net.pick[z])
+    for a in range(QF * QF):
+        line = z_sum([load[a * QF], load[a * QF + QF - 1]], lanes)
+        load[a * QF] = line[0]
+        load[a * QF + QF - 1] = line[1]
     local_sum(load, QF, range(QF - 1))
 
     def each(q, body):
@@ -550,17 +555,17 @@
     for n, full, part in ((1, flux, cflux), (2, mass, cmass)):
         for copy in arriving[n * QF : (n + 1) * QF]:
             copy.wait()
-        for x in range(QF):
-            for y in range(QF):
-                for h, values in enumerate(read_planes(n, x, y)):
-                    place = slice(h * tile, (h + 1) * tile)
-                    for z in range(QF):
-                        weight = float(FINE_W[x] * FINE_W[y] * FINE_W[z])
-                        full[(x * QF + y) * QF + z, place, :] = weight * values[z]
-                        if x in pick and y in pick and z in pick:
-                            i, j, k = pick[x], pick[y], pick[z]
-                            weight = float(COARSE_W[i] * COARSE_W[j] * COARSE_W[k])
-                            part[(i * QC + j) * QC + k, place, :] = weight * values[z]
+        read_planes(n, full)
+        for z in range(QF):
+            for x in range(QF):
+                for y in range(QF):
+                    p = (x * QF + y) * QF + z
+                    value = permuted(full[p], net.pick[z])
+                    full[p] = float(FINE_W[x] * FINE_W[y] * FINE_W[z]) * value
+                    if x in pick and y in pick and z in pick:
+                        i, j, k = pick[x], pick[y], pick[z]
+                        weight = float(COARSE_W[i] * COARSE_W[j] * COARSE_W[k])
+                        part[(i * QC + j) * QC + k] = weight * value
 
     local_diag(inv, flux, mass, FINE_D, lanes)
     local_sum(inv, QF, inner_f)
@@ -624,12 +629,12 @@
     line = start_line(0, True, sum_first, sum_second)
 
     finish_exchange(fine, 5, [(b2, QF)], f_w1, [scaled])
+    line = start_line(0, False, *finish_line(0, True, line))
     apply_fine(b2, power)
     restrict(power, rw2, False)
     local_sum(rw2, QC, inner_c)
     c_3 = start_exchange(rough, 3, [(rw2, QC)])
 
-    line = start_line(0, False, *finish_line(0, True, line))
     finish_exchange(rough, 2, [(cpow_2, QC), (rw1, QC)], c_2, [cscaled, keep])
     csum_first = squares(QC, lambda p: cpow[p])
     csum_second = squares(QC, lambda p: cpow_2[p])
@@ -661,21 +666,25 @@
     finish_exchange(rough, 5, [(cw1, QC)], c_5, [cscaled])
     each(QC, store(ccor, lambda p: ccor[p] + cscale[2] * cw1[p]))
 
-    def write_planes(dst, q, x, y, values, lane_net):
-        for h in range(subs // tile):
-            rows = slice(h * tile, (h + 1) * tile)
-            for v, block in enumerate(lane_net.merge([value[rows] for value in values])):
-                for e in range(group):
-                    part = block[e * ey : (e + 1) * ey]
-                    dst[v, x, h * group + e, pl.ds(y, ey, stride=q), :] = part
+    def write_planes(dst, planes, q, lane_net):
+        for x in range(q):
+            for y in range(q):
+                for h in range(subs // tile):
+                    rows = slice(h * tile, (h + 1) * tile)
+                    placed = [planes[(x * q + y) * q + z, rows, :] for z in range(q)]
+                    for v, block in enumerate(lane_net.unmix(placed)):
+                        for e in range(group):
+                            part = block[e * ey : (e + 1) * ey]
+                            dst[v, x, h * group + e, pl.ds(y, ey, stride=q), :] = part
 
     leaving = []
     cnet = Lanes(QC, tile, ez)
-    for x in range(QC):
-        for y in range(QC):
-            values = [ccor[(x * QC + y) * QC + z] for z in range(QC)]
-            write_planes(cresult, QC, x, y, values, cnet)
-        for v in range(QC):
+    for z in range(QC):
+        for a in range(QC * QC):
+            tmp_b[a * QC + z] = permuted(ccor[a * QC + z], cnet.place[z])
+    write_planes(cresult, tmp_b, QC, cnet)
+    for v in range(QC):
+        for x in range(QC):
             copy = pltpu.make_async_copy(
                 cresult.at[v, x], cor_hbm.at[:, x, :, v * ez : (v + 1) * ez], cor_sem.at[v, x]
             )
@@ -691,11 +700,14 @@
             line = dense(INTERP, [tmp_a[(x * QC + i) * QC + z] for i in range(QC)])
             for i in range(QF):
                 tmp_b[(x * QF + i) * QC + z] = line[i]
-        for y in range(QF):
-            line = dense(INTERP, [tmp_b[(x * QF + y) * QC + i] for i in range(QC)])
-            values = [smooth[(x * QF + y) * QF + z] + line[z] for z in range(QF)]
-            write_planes(result, QF, x, y, values, net)
-        for v in range(QF):
+    for z in range(QF):
+        for a in range(QF * QF):
+            p = a * QF + z
+            lifted = dense(INTERP[z : z + 1], [tmp_b[a * QC + i] for i in range(QC)])[0]
+            smooth[p] = permuted(smooth[p] + lifted, net.place[z])
+    write_planes(result, smooth, QF, net)
+    for v in range(QF):
+        for x in range(QF):
             copy = pltpu.make_async_copy(
                 result.at[v, x], out_hbm.at[:, x, :, v * ez : (v + 1) * ez], out_sem.at[v, x]
             )
@@ -747,11 +759,11 @@
             jax.ShapeDtypeStruct((ex, QF, py, pz), f32),
             jax.ShapeDtypeStruct((ex, QC, ey * QC, ez * QC), f32),
         ),
-        in_specs=[anywhere] * 3,
+        in_specs=[pl.BlockSpec(memory_space=pltpu.HBM)] * 3,
         out_specs=(anywhere, anywhere),
         scratch_shapes=scratch,
         compiler_params=pltpu.CompilerParams(
-            collective_id=0, has_side_effects=True, vmem_limit_bytes=40 * 1024 * 1024
+            collective_id=0, has_side_effects=True, vmem_limit_bytes=52 * 1024 * 1024
         ),
     )(source, conductivity, absorption)
     return out.reshape(source.shape), cor.reshape(ex * QC, ey * QC, ez * QC)

time: 52.9 us -> 47.8 us (0.904)
  local copies, waits for them, and re-layouts: 5.6 us -> 1.75 us
  Pallas kernels: 46.4 us -> 45.2 us
    unnamed x8 -> x2, local copies, waits for them, and re-layouts: 5.6 us -> 1.75 us
    pallas_call x1, Pallas kernels: 46.4 us -> 45.2 us  [on_device(): pl.pallas_call(functools.partial(kernel, nx, ny), out_shape=(jax.ShapeDty...]
where the time goes in v2:
time: 47.8 us; the launch traced here: 47.6 us
  Pallas kernels  45.2 us (95%)
  local copies, waits for them, and re-layouts  1.75 us (4%)
  between operations  0.64 us (1%)
    pallas_call x1, Pallas kernels, on_device(): pl.pallas_call(functools.partial(kernel, nx, ny), out_shape=(jax.ShapeDty...  45.2 us
    unnamed x2, local copies, waits for them, and re-layouts  1.75 us

profile of v2, /device:TPU:0, one launch (start us, length us, event | category | flops | bytes accessed | tf_op | source)
XLA Modules:
  0.0 47.6 jit_solution(17033894234498703975)
XLA Ops:
  0.6 45.2 %shard_map.50 = (f32[4,5,20,640]{3,2,1,0:T(8,128)S(1)}, f32[4,3,12,384]{3,2,1,0:T(8,128)S(1)}) custom-call(f32[20,20,640]{2,1,0:T(8,128)} %src_hbm.1, f32[20,20,640]{2,1,0:T(8,128)} %cond_hbm.1, f32[20,20,640]{2,1,0:T(8,128)} %abs_hbm.1), custom_call_target="tpu_custom_call" | custom-call | tf_op jit(solution)/shard_map/pallas_call | solution.py:756
  45.9 1.0 %copy.7 = f32[20,20,640]{2,1,0:T(8,128)} copy(f32[20,20,640]{2,1,0:T(8,128)S(1)} %bitcast.2) | data formatting | bytes 2048000
  46.9 0.7 %copy.8 = f32[12,12,384]{2,1,0:T(8,128)} copy(f32[12,12,384]{2,1,0:T(8,128)S(1)} %bitcast.3) | data formatting | bytes 442368

commit v3 on v2

--- a/solution.py
+++ b/solution.py
@@ -109,6 +109,24 @@
     return out
 
 
+def centrosym(table, u):
+    n = len(u)
+    half = n // 2
+    even = [u[j] + u[n - 1 - j] for j in range(half)]
+    odd = [u[j] - u[n - 1 - j] for j in range(half)]
+    out = [None] * n
+    for i in range(half):
+        s = [(table[i, j] + table[i, n - 1 - j]) / 2 for j in range(half)]
+        t = [[(table[i, j] - table[i, n - 1 - j]) / 2 for j in range(half)]]
+        p = dense(np.array([s + [table[i, half]]]), even + [u[half]])[0]
+        q = dense(np.array(t), odd)[0]
+        out[i] = p + q
+        out[n - 1 - i] = p - q
+    middle = np.array([[table[half, j] for j in range(half + 1)]])
+    out[half] = dense(middle, even + [u[half]])[0]
+    return out
+
+
 def plane_starts(q, axis, a, b):
     strides = (q * q, q, 1)
     other = [s for k, s in enumerate(strides) if k != axis]
@@ -122,22 +140,22 @@
     return line
 
 
-def local_op(src, dst, flux, mass, table, lanes):
+def local_op(src, dst, flux, mass, table, lanes, between=None):
     q = table.shape[0]
 
-    def lines(axis, a):
-        def read(b):
-            start, step = plane_starts(q, axis, a, b)
+    def lines(axis, places):
+        def read(n):
+            start, step = plane_starts(q, axis, *places[n])
             u = [src[start + step * i] for i in range(q)]
             base = None if axis == 0 else [dst[start + step * i] for i in range(q)]
             return u, base
 
         ahead = read(0)
-        for b in range(q):
+        for n in range(len(places)):
             u, base = ahead
-            if b + 1 < q:
-                ahead = read(b + 1)
-            start, step = plane_starts(q, axis, a, b)
+            if n + 1 < len(places):
+                ahead = read(n + 1)
+            start, step = plane_starts(q, axis, *places[n])
             g = antisym(table, u)
             g = [flux[start + step * i] * g[i] for i in range(q)]
             r = antisym(table.T, g)
@@ -152,10 +170,13 @@
 
         @pl.loop(0, q)
         def _(a, axis=axis):
-            lines(axis, a)
-
-    for a in range(q):
-        lines(2, a)
+            lines(axis, [(a, b) for b in range(q)])
+
+    lines(2, [(a, b) for b in (0, q - 1) for a in range(q)])
+    if between is not None:
+        between()
+    lines(2, [(a, b) for b in range(1, q - 1) for a in (0, q - 1)])
+    lines(2, [(a, b) for b in range(1, q - 1) for a in range(1, q - 1)])
 
 
 def local_diag(dst, flux, mass, table, lanes):
@@ -165,7 +186,7 @@
     def lines(axis, a):
         for b in range(q):
             start, step = plane_starts(q, axis, a, b)
-            r = dense(square, [flux[start + step * i] for i in range(q)])
+            r = centrosym(square, [flux[start + step * i] for i in range(q)])
             for i in range(q):
                 base = mass if axis == 0 else dst
                 r[i] = base[start + step * i] + r[i]
@@ -294,19 +315,27 @@
     def shifted(plane, shift):
         return pltpu.roll(plane, shift % subs, 0)
 
-    def local_sum(ref, q, zs):
+    def sum_x(ref, q, zs, ys):
         last = q - 1
         for z in zs:
-            for y in range(q):
+            for y in ys:
                 p, r = y * q + z, (last * q + y) * q + z
                 lo, hi = ref[p], ref[r]
                 ref[p] = jnp.where(first_x, lo, lo + shifted(hi, ey))
                 ref[r] = jnp.where(last_x, hi, hi + shifted(lo, -ey))
+
+    def sum_y(ref, q, zs):
+        last = q - 1
+        for z in zs:
             for x in range(q):
                 p, r = x * q * q + z, (x * q + last) * q + z
                 lo, hi = ref[p], ref[r]
                 ref[p] = jnp.where(first_y, lo, lo + shifted(hi, 1))
                 ref[r] = jnp.where(last_y, hi, hi + shifted(lo, -1))
+
+    def local_sum(ref, q, zs):
+        sum_x(ref, q, zs, range(q))
+        sum_y(ref, q, zs)
 
     def edge(dx, dy, q):
         xs = range(q) if dx == 0 else [0 if dx < 0 else q - 1]
@@ -324,10 +353,11 @@
 
     pending = []
 
-    def start_exchange(level, stage, fields):
+    def start_exchange(level, stage, fields, ways=range(len(DIRS))):
         send, recv, sems = level
         copies = []
-        for d, (dx, dy) in enumerate(DIRS):
+        for d in ways:
+            dx, dy = DIRS[d]
             at = 0
             for ref, q in fields:
                 planes, count, rows = edge(dx, dy, q)
@@ -539,6 +569,18 @@
     def apply_fine(src, dst):
         local_op(src, dst, flux, mass, FINE_D, lanes)
 
+    def apply_and_send(src, dst, stage):
+        copies = []
+
+        def first_part():
+            sum_x(dst, QF, inner_f, (0, QF - 1))
+            copies.extend(start_exchange(fine, stage, [(dst, QF)], range(6)))
+
+        local_op(src, dst, flux, mass, FINE_D, lanes, first_part)
+        sum_x(dst, QF, inner_f, range(1, QF - 1))
+        sum_y(dst, QF, inner_f)
+        return copies + start_exchange(fine, stage, [(dst, QF)], range(6, len(DIRS)))
+
     def apply_coarse(src, dst):
         local_op(src, dst, cflux, cmass, COARSE_D, lanes)
 
@@ -580,16 +622,12 @@
     interior(inv, QF, invert)
 
     finish_exchange(fine, 0, [(load, QF)], f_load, [keep])
-    apply_fine(load, power)
-    local_sum(power, QF, inner_f)
-    f_power = start_exchange(fine, 2, [(power, QF)])
+    f_power = apply_and_send(load, power, 2)
     interior(power, QF, scaled)
 
     finish_exchange(fine, 1, [(inv, QF)], f_diag, [invert])
     each(QF, store(b0, lambda p: inv[p] * load[p]))
-    apply_fine(b0, b1)
-    local_sum(b1, QF, inner_f)
-    f_w0 = start_exchange(fine, 3, [(b1, QF)])
+    f_w0 = apply_and_send(b0, b1, 3)
 
     local_sum(b1, QF, [QF - 1])
     restrict(b1, rw0, True)
@@ -603,15 +641,11 @@
     interior(cpow, QC, cscaled)
 
     finish_exchange(fine, 2, [(power, QF)], f_power, [scaled])
-    apply_fine(power, power_2)
-    local_sum(power_2, QF, inner_f)
-    f_power_2 = start_exchange(fine, 4, [(power_2, QF)])
+    f_power_2 = apply_and_send(power, power_2, 4)
     interior(power_2, QF, scaled)
 
     finish_exchange(fine, 3, [(b1, QF)], f_w0, [scaled])
-    apply_fine(b1, b2)
-    local_sum(b2, QF, inner_f)
-    f_w1 = start_exchange(fine, 5, [(b2, QF)])
+    f_w1 = apply_and_send(b1, b2, 5)
 
     local_sum(b2, QF, [QF - 1])
     restrict(b2, rw1, True)
@@ -663,6 +697,10 @@
     cscale = coefficients(inverse_estimate(*finish_line(1, False, cline)))
     each(QC, store(ccor, lambda p: cscale[0] * cb[p] + cscale[1] * cw0[p]))
 
+    for copy in pending:
+        copy.wait_send()
+    pending.clear()
+
     finish_exchange(rough, 5, [(cw1, QC)], c_5, [cscaled])
     each(QC, store(ccor, lambda p: ccor[p] + cscale[2] * cw1[p]))
 
@@ -675,7 +713,7 @@
                     for v, block in enumerate(lane_net.unmix(placed)):
                         for e in range(group):
                             part = block[e * ey : (e + 1) * ey]
-                            dst[v, x, h * group + e, pl.ds(y, ey, stride=q), :] = part
+                            dst[v, (h * group + e) * q + x, pl.ds(y, ey, stride=q), :] = part
 
     leaving = []
     cnet = Lanes(QC, tile, ez)
@@ -684,12 +722,11 @@
             tmp_b[a * QC + z] = permuted(ccor[a * QC + z], cnet.place[z])
     write_planes(cresult, tmp_b, QC, cnet)
     for v in range(QC):
-        for x in range(QC):
-            copy = pltpu.make_async_copy(
-                cresult.at[v, x], cor_hbm.at[:, x, :, v * ez : (v + 1) * ez], cor_sem.at[v, x]
-            )
-            copy.start()
-            leaving.append(copy)
+        copy = pltpu.make_async_copy(
+            cresult.at[v], cor_hbm.at[:, :, v * ez : (v + 1) * ez], cor_sem.at[v]
+        )
+        copy.start()
+        leaving.append(copy)
     for y in range(QC):
         for z in range(QC):
             line = dense(INTERP, [ccor[i * QC * QC + y * QC + z] for i in range(QC)])
@@ -707,15 +744,25 @@
             smooth[p] = permuted(smooth[p] + lifted, net.place[z])
     write_planes(result, smooth, QF, net)
     for v in range(QF):
-        for x in range(QF):
-            copy = pltpu.make_async_copy(
-                result.at[v, x], out_hbm.at[:, x, :, v * ez : (v + 1) * ez], out_sem.at[v, x]
-            )
-            copy.start()
-            leaving.append(copy)
+        copy = pltpu.make_async_copy(
+            result.at[v], out_hbm.at[:, :, v * ez : (v + 1) * ez], out_sem.at[v]
+        )
+        copy.start()
+        leaving.append(copy)
     for copy in pending:
         copy.wait_send()
     for copy in leaving:
+        copy.wait()
+
+
+def hand_over(out_ref, cor_ref, out_hbm, cor_hbm, sems):
+    copies = [
+        pltpu.make_async_copy(out_ref, out_hbm, sems.at[0]),
+        pltpu.make_async_copy(cor_ref, cor_hbm, sems.at[1]),
+    ]
+    for copy in copies:
+        copy.start()
+    for copy in copies:
         copy.wait()
 
 
@@ -731,8 +778,8 @@
     coarse_rows = -(-2 * QC * (QC - 1) * face // 8) * 8
     scratch = [
         pltpu.VMEM((3, QF, px, py, ez), f32),
-        pltpu.VMEM((QF, QF, ex, py, ez), f32),
-        pltpu.VMEM((QC, QC, ex, ey * QC, ez), f32),
+        pltpu.VMEM((QF, px, py, ez), f32),
+        pltpu.VMEM((QC, ex * QC, ey * QC, ez), f32),
         *[pltpu.VMEM((QF**3, subs, ez), f32)] * 10,
         pltpu.VMEM((14, QC**3, subs, ez), f32),
         pltpu.VMEM((QF * QF * QC, subs, ez), f32),
@@ -744,8 +791,8 @@
         pltpu.VMEM((2, 8, ez), f32),
         pltpu.VMEM((2, ny, 8, ez), f32),
         pltpu.SemaphoreType.DMA((3, QF)),
-        pltpu.SemaphoreType.DMA((QF, QF)),
-        pltpu.SemaphoreType.DMA((QC, QC)),
+        pltpu.SemaphoreType.DMA((QF,)),
+        pltpu.SemaphoreType.DMA((QC,)),
         pltpu.SemaphoreType.DMA((2, FINE_STAGES, dirs)),
         pltpu.SemaphoreType.DMA((2, COARSE_STAGES, dirs)),
         pltpu.SemaphoreType.DMA((2, 2, longest)),
@@ -756,8 +803,8 @@
     out, cor = pl.pallas_call(
         functools.partial(kernel, nx, ny),
         out_shape=(
-            jax.ShapeDtypeStruct((ex, QF, py, pz), f32),
-            jax.ShapeDtypeStruct((ex, QC, ey * QC, ez * QC), f32),
+            jax.ShapeDtypeStruct(source.shape, f32),
+            jax.ShapeDtypeStruct((ex * QC, ey * QC, ez * QC), f32),
         ),
         in_specs=[pl.BlockSpec(memory_space=pltpu.HBM)] * 3,
         out_specs=(anywhere, anywhere),
@@ -766,7 +813,14 @@
             collective_id=0, has_side_effects=True, vmem_limit_bytes=52 * 1024 * 1024
         ),
     )(source, conductivity, absorption)
-    return out.reshape(source.shape), cor.reshape(ex * QC, ey * QC, ez * QC)
+    return pl.pallas_call(
+        hand_over,
+        out_shape=(out, cor),
+        in_specs=[anywhere] * 2,
+        out_specs=(pl.BlockSpec(memory_space=pltpu.HBM),) * 2,
+        scratch_shapes=[pltpu.SemaphoreType.DMA((2,))],
+        compiler_params=pltpu.CompilerParams(vmem_limit_bytes=1024 * 1024),
+    )(out, cor)
 
 
 def solution(mesh):

time: 47.8 us -> 45.9 us (0.960)
  local copies, waits for them, and re-layouts: 1.75 us -> 0 us
    unnamed x2 -> x0, local copies, waits for them, and re-layouts: 1.75 us -> none
    pallas_call x1, Pallas kernels: 45.2 us -> 43.9 us  [on_device(): pl.pallas_call(functools.partial(kernel, nx, ny), out_shape=(jax.ShapeDty...]
    pallas_call x0 -> x1, Pallas kernels: none -> 1.14 us  [on_device(): pl.pallas_call(hand_over, out_shape=(out, cor), in_specs=[anywhere] * 2,...]
where the time goes in v3:
time: 45.9 us; the launch traced here: 45.7 us
  Pallas kernels  45.1 us (98%)
  between operations  0.64 us (1%)
    pallas_call x1, Pallas kernels, on_device(): pl.pallas_call(functools.partial(kernel, nx, ny), out_shape=(jax.ShapeDty...  43.9 us
    pallas_call x1, Pallas kernels, on_device(): pl.pallas_call(hand_over, out_shape=(out, cor), in_specs=[anywhere] * 2,...  1.14 us

profile of v3, /device:TPU:0, one launch (start us, length us, event | category | flops | bytes accessed | tf_op | source)
XLA Modules:
  0.0 45.7 jit_solution(8441452236900482765)
XLA Ops:
  0.6 43.9 %shard_map.50 = (f32[20,20,640]{2,1,0:T(8,128)S(1)}, f32[12,12,384]{2,1,0:T(8,128)S(1)}) custom-call(f32[20,20,640]{2,1,0:T(8,128)} %src_hbm.1, f32[20,20,640]{2,1,0:T(8,128)} %cond_hbm.1, f32[20,20,640]{2,1,0:T(8,128)} %abs_hbm.1), custom_call_target="tpu_custom_call" | custom-call | tf_op jit(solution)/shard_map/pallas_call | solution.py:803
  44.6 1.1 %shard_map.51 = (f32[20,20,640]{2,1,0:T(8,128)}, f32[12,12,384]{2,1,0:T(8,128)}) custom-call(f32[20,20,640]{2,1,0:T(8,128)S(1)} %get-tuple-element.4.out_ref, f32[12,12,384]{2,1,0:T(8,128)S(1)} %get-tuple-element.5.cor_ref), custom_call_target="tpu_custom_call" | custom-call | tf_op jit(solution)/shard_map/pallas_call | solution.py:816

commit v4 on v3

--- a/solution.py
+++ b/solution.py
@@ -71,27 +71,66 @@
 CHEB = chebyshev_coefficients()
 
 
-def antisym(table, u):
+def row_scales(table):
+    n = table.shape[0]
+    half = n // 2
+    scale = np.ones(n)
+    for i in range(half):
+        scale[i] = scale[n - 1 - i] = 2.0 / (table[i, 0] + table[i, n - 1])
+    scale[half] = 1.0 / table[half, 0]
+    return scale
+
+
+def halves(table):
+    n = table.shape[0]
+    half = n // 2
+    scaled = row_scales(table)[:, None] * table
+    even = [[(scaled[i, j] + scaled[i, n - 1 - j]) / 2 for j in range(half)] for i in range(half)]
+    odd = [[(scaled[i, j] - scaled[i, n - 1 - j]) / 2 for j in range(half)] for i in range(half)]
+    middle = [scaled[half, j] for j in range(half)]
+    return even, odd, middle
+
+
+def combine(weights, terms):
+    acc = None
+    for w, t in zip(weights, terms):
+        w = float(w)
+        if abs(w) < 1e-14:
+            continue
+        term = t if abs(w - 1.0) < 1e-12 else w * t
+        acc = term if acc is None else acc + term
+    return acc
+
+
+def derive(table, u):
     n = len(u)
     half = n // 2
-    even = [u[j] + u[n - 1 - j] for j in range(half)]
-    odd = [u[j] - u[n - 1 - j] for j in range(half)]
+    even, odd, middle = halves(table)
+    twice = u[half] + u[half]
+    a = [u[j] + u[n - 1 - j] - twice for j in range(half)]
+    o = [u[j] - u[n - 1 - j] for j in range(half)]
     out = [None] * n
     for i in range(half):
-        p = float(table[i, half]) * u[half]
-        q = None
-        for j in range(half):
-            s = (table[i, j] + table[i, n - 1 - j]) / 2
-            t = (table[i, j] - table[i, n - 1 - j]) / 2
-            p = p + float(s) * even[j]
-            q = float(t) * odd[j] if q is None else q + float(t) * odd[j]
-        out[i] = q + p
-        out[n - 1 - i] = q - p
-    mid = None
+        p, q = combine(even[i], a), combine(odd[i], o)
+        out[i], out[n - 1 - i] = q + p, q - p
+    out[half] = combine(middle, o)
+    return out
+
+
+def derive_back(table, g):
+    n = len(g)
+    half = n // 2
+    even, odd, middle = halves(table)
+    plus = [g[i] + g[n - 1 - i] for i in range(half)]
+    minus = [g[i] - g[n - 1 - i] for i in range(half)]
+    out = [None] * n
+    total = None
     for j in range(half):
-        term = float(table[half, j]) * odd[j]
-        mid = term if mid is None else mid + term
-    out[half] = mid
+        a = combine([even[i][j] for i in range(half)], minus)
+        o = combine([odd[i][j] for i in range(half)] + [middle[j]], plus + [g[half]])
+        out[j], out[n - 1 - j] = a + o, a - o
+        total = a if total is None else total + a
+    out[half] = -2.0 * total
     return out
 
 
@@ -140,43 +179,56 @@
     return line
 
 
-def local_op(src, dst, flux, mass, table, lanes, between=None):
+def operator_lines(src, dst, flux, mass, table, lanes, axis, places):
     q = table.shape[0]
 
-    def lines(axis, places):
-        def read(n):
-            start, step = plane_starts(q, axis, *places[n])
-            u = [src[start + step * i] for i in range(q)]
-            base = None if axis == 0 else [dst[start + step * i] for i in range(q)]
-            return u, base
-
-        ahead = read(0)
-        for n in range(len(places)):
-            u, base = ahead
-            if n + 1 < len(places):
-                ahead = read(n + 1)
-            start, step = plane_starts(q, axis, *places[n])
-            g = antisym(table, u)
-            g = [flux[start + step * i] * g[i] for i in range(q)]
-            r = antisym(table.T, g)
-            for i in range(q):
-                r[i] = (mass[start + step * i] * u[i] if base is None else base[i]) + r[i]
-            if axis == 2:
-                r = z_sum(r, lanes)
-            for i in range(q):
-                dst[start + step * i] = r[i]
-
-    for axis in range(2):
-
-        @pl.loop(0, q)
-        def _(a, axis=axis):
-            lines(axis, [(a, b) for b in range(q)])
-
-    lines(2, [(a, b) for b in (0, q - 1) for a in range(q)])
+    def read(n):
+        start, step = plane_starts(q, axis, *places[n])
+        u = [src[start + step * i] for i in range(q)]
+        base = None if axis == 0 else [dst[start + step * i] for i in range(q)]
+        return u, base
+
+    ahead = read(0)
+    for n in range(len(places)):
+        u, base = ahead
+        if n + 1 < len(places):
+            ahead = read(n + 1)
+        start, step = plane_starts(q, axis, *places[n])
+        g = derive(table, u)
+        g = [flux[axis, start + step * i] * g[i] for i in range(q)]
+        r = derive_back(table, g)
+        for i in range(q):
+            r[i] = (mass[start + step * i] * u[i] if base is None else base[i]) + r[i]
+        if axis == 2:
+            r = z_sum(r, lanes)
+        for i in range(q):
+            dst[start + step * i] = r[i]
+
+
+def operator_start(src, dst, flux, mass, table, lanes):
+    q = table.shape[0]
+
+    @pl.loop(1, q - 1)
+    def _(y):
+        operator_lines(src, dst, flux, mass, table, lanes, 0, [(y, z) for z in range(q)])
+
+
+def local_op(src, dst, flux, mass, table, lanes, between=None, started=False):
+    q = table.shape[0]
+    run = functools.partial(operator_lines, src, dst, flux, mass, table, lanes)
+    if not started:
+        operator_start(src, dst, flux, mass, table, lanes)
+    run(0, [(y, z) for y in (0, q - 1) for z in range(q)])
+
+    @pl.loop(0, q)
+    def _(a):
+        run(1, [(a, b) for b in range(q)])
+
+    run(2, [(a, b) for b in (0, q - 1) for a in range(q)])
     if between is not None:
         between()
-    lines(2, [(a, b) for b in range(1, q - 1) for a in (0, q - 1)])
-    lines(2, [(a, b) for b in range(1, q - 1) for a in range(1, q - 1)])
+    run(2, [(a, b) for b in range(1, q - 1) for a in (0, q - 1)])
+    run(2, [(a, b) for b in range(1, q - 1) for a in range(1, q - 1)])
 
 
 def local_diag(dst, flux, mass, table, lanes):
@@ -247,11 +299,9 @@
     src_hbm,
     cond_hbm,
     abs_hbm,
-    out_hbm,
-    cor_hbm,
-    stored,
     result,
     cresult,
+    stored,
     load,
     inv,
     power,
@@ -260,6 +310,8 @@
     b1,
     b2,
     flux,
+    fluxes,
+    cfluxes,
     mass,
     smooth,
     coarse,
@@ -274,8 +326,6 @@
     line_y_send,
     line_y,
     in_sem,
-    out_sem,
-    cor_sem,
     fine_sems,
     coarse_sems,
     line_send_sem,
@@ -377,7 +427,7 @@
             copies.append(copy)
         return copies
 
-    def finish_exchange(level, stage, fields, copies, finals):
+    def finish_exchange(level, stage, fields, copies, finals, meanwhile=None):
         _, recv, _ = level
         for d in reversed(range(len(DIRS))):
             dx, dy = DIRS[d]
@@ -388,24 +438,33 @@
                 for p in planes:
                     ref[p, rows, :] = ref[p, rows, :] + recv[stage, d, at : at + count, :]
                     at += count
+            if d == len(DIRS) - 2:
+                for (ref, q), final in zip(fields, finals):
+                    boundary(ref, ref, q, final, range(1, q - 1))
+                if meanwhile is not None:
+                    meanwhile()
         pending.extend(copies)
         for (ref, q), final in zip(fields, finals):
-            for x in range(q):
-                for y in range(q):
-                    if x in (0, q - 1) or y in (0, q - 1):
-                        p = (x * q + y) * q
-                        for z in range(q - 1):
-                            value = final(p + z, ref[p + z])
-                            ref[p + z] = value
-                            if z == 0:
-                                ref[p + q - 1] = pltpu.roll(value, lanes - 1, 1)
-
-    def interior(ref, q, final):
+            boundary(ref, ref, q, final, (0, q - 1))
+
+    def boundary(ref, dst, q, final, ys):
+        for x in range(q):
+            for y in ys:
+                if x in (0, q - 1) or y in (0, q - 1):
+                    p = (x * q + y) * q
+                    for z in range(q - 1):
+                        value = final(p + z, ref[p + z])
+                        dst[p + z] = value
+                        if z == 0:
+                            dst[p + q - 1] = pltpu.roll(value, lanes - 1, 1)
+
+    def interior(ref, q, final, dst=None):
+        dst = ref if dst is None else dst
         for x in range(1, q - 1):
             for y in range(1, q - 1):
                 for z in range(q):
                     p = (x * q + y) * q + z
-                    ref[p] = final(p, ref[p])
+                    dst[p] = final(p, ref[p])
 
     fine = (fine_send, fine_recv, fine_sems)
     rough = (coarse_send, coarse_recv, coarse_sems)
@@ -490,11 +549,10 @@
         rw1,
         rw2,
         crhs,
-        cb,
         cw0,
         cw1,
         ccor,
-    ) = [coarse.at[i] for i in range(14)]
+    ) = [coarse.at[i] for i in range(13)]
 
     for copy in arriving[:QF]:
         copy.wait()
@@ -566,23 +624,35 @@
                 for i in range(QC):
                     dst[a * QC * QC + c * QC + i] = line[i]
 
-    def apply_fine(src, dst):
-        local_op(src, dst, flux, mass, FINE_D, lanes)
-
-    def apply_and_send(src, dst, stage):
+    def scaled_fluxes(flux, scaled, table):
+        q = table.shape[0]
+        square = 1.0 / row_scales(table) ** 2
+
+        for x in range(q):
+            for y in range(q):
+                for z in range(q):
+                    p = (x * q + y) * q + z
+                    value = flux[p]
+                    for axis, i in enumerate((x, y, z)):
+                        scaled[axis, p] = float(square[i]) * value
+
+    def start_apply(src, dst):
+        return lambda: operator_start(src, dst, fluxes, mass, FINE_D, lanes)
+
+    def apply_and_send(src, dst, stage, started=True):
         copies = []
 
         def first_part():
             sum_x(dst, QF, inner_f, (0, QF - 1))
             copies.extend(start_exchange(fine, stage, [(dst, QF)], range(6)))
 
-        local_op(src, dst, flux, mass, FINE_D, lanes, first_part)
+        local_op(src, dst, fluxes, mass, FINE_D, lanes, first_part, started)
         sum_x(dst, QF, inner_f, range(1, QF - 1))
         sum_y(dst, QF, inner_f)
         return copies + start_exchange(fine, stage, [(dst, QF)], range(6, len(DIRS)))
 
     def apply_coarse(src, dst):
-        local_op(src, dst, cflux, cmass, COARSE_D, lanes)
+        local_op(src, dst, cfluxes, cmass, COARSE_D, lanes)
 
     keep = lambda p, v: v
     invert = lambda p, v: 1.0 / v
@@ -619,14 +689,22 @@
     local_diag(cinv, cflux, cmass, COARSE_D, lanes)
     local_sum(cinv, QC, inner_c)
     c_0 = start_exchange(rough, 0, [(cinv, QC), (rload, QC)])
+    scaled_fluxes(flux, fluxes, FINE_D)
+    scaled_fluxes(cflux, cfluxes, COARSE_D)
     interior(inv, QF, invert)
 
-    finish_exchange(fine, 0, [(load, QF)], f_load, [keep])
+    finish_exchange(fine, 0, [(load, QF)], f_load, [keep], start_apply(load, power))
     f_power = apply_and_send(load, power, 2)
     interior(power, QF, scaled)
 
-    finish_exchange(fine, 1, [(inv, QF)], f_diag, [invert])
-    each(QF, store(b0, lambda p: inv[p] * load[p]))
+    interior(load, QF, scaled, b0)
+
+    def start_b0():
+        boundary(load, b0, QF, scaled, range(1, QF - 1))
+        operator_start(b0, b1, fluxes, mass, FINE_D, lanes)
+
+    finish_exchange(fine, 1, [(inv, QF)], f_diag, [invert], start_b0)
+    boundary(load, b0, QF, scaled, (0, QF - 1))
     f_w0 = apply_and_send(b0, b1, 3)
 
     local_sum(b1, QF, [QF - 1])
@@ -640,11 +718,11 @@
     c_1 = start_exchange(rough, 1, [(cpow, QC), (rw0, QC)])
     interior(cpow, QC, cscaled)
 
-    finish_exchange(fine, 2, [(power, QF)], f_power, [scaled])
+    finish_exchange(fine, 2, [(power, QF)], f_power, [scaled], start_apply(power, power_2))
     f_power_2 = apply_and_send(power, power_2, 4)
     interior(power_2, QF, scaled)
 
-    finish_exchange(fine, 3, [(b1, QF)], f_w0, [scaled])
+    finish_exchange(fine, 3, [(b1, QF)], f_w0, [scaled], start_apply(b1, b2))
     f_w1 = apply_and_send(b1, b2, 5)
 
     local_sum(b2, QF, [QF - 1])
@@ -662,9 +740,13 @@
     sum_second = squares(QF, lambda p: power_2[p])
     line = start_line(0, True, sum_first, sum_second)
 
-    finish_exchange(fine, 5, [(b2, QF)], f_w1, [scaled])
-    line = start_line(0, False, *finish_line(0, True, line))
-    apply_fine(b2, power)
+    finish_exchange(fine, 5, [(b2, QF)], f_w1, [scaled], start_apply(b2, power))
+    across = []
+
+    def forward():
+        across.extend(start_line(0, False, *finish_line(0, True, line)))
+
+    local_op(b2, power, fluxes, mass, FINE_D, lanes, forward, True)
     restrict(power, rw2, False)
     local_sum(rw2, QC, inner_c)
     c_3 = start_exchange(rough, 3, [(rw2, QC)])
@@ -673,17 +755,17 @@
     csum_first = squares(QC, lambda p: cpow[p])
     csum_second = squares(QC, lambda p: cpow_2[p])
     cline = start_line(1, True, csum_first, csum_second)
-    scale = coefficients(inverse_estimate(*finish_line(0, False, line)))
+    scale = coefficients(inverse_estimate(*finish_line(0, False, across)))
     each(
         QF,
         store(smooth, lambda p: scale[0] * b0[p] + scale[1] * b1[p] + scale[2] * b2[p]),
     )
     each(QC, store(crhs, lambda p: rload[p] - (scale[0] * rw0[p] + scale[1] * rw1[p])))
 
-    finish_exchange(rough, 3, [(rw2, QC)], c_3, [keep])
-    each(QC, store(crhs, lambda p: crhs[p] - scale[2] * rw2[p]))
-    each(QC, store(cb, lambda p: cinv[p] * crhs[p]))
-    apply_coarse(cb, cw0)
+    first = lambda p, v: cinv[p] * (crhs[p] - scale[2] * v)
+    interior(rw2, QC, first)
+    finish_exchange(rough, 3, [(rw2, QC)], c_3, [first])
+    apply_coarse(rw2, cw0)
     local_sum(cw0, QC, inner_c)
     c_4 = start_exchange(rough, 4, [(cw0, QC)])
     interior(cw0, QC, cscaled)
@@ -695,7 +777,7 @@
     c_5 = start_exchange(rough, 5, [(cw1, QC)])
     interior(cw1, QC, cscaled)
     cscale = coefficients(inverse_estimate(*finish_line(1, False, cline)))
-    each(QC, store(ccor, lambda p: cscale[0] * cb[p] + cscale[1] * cw0[p]))
+    each(QC, store(ccor, lambda p: cscale[0] * rw2[p] + cscale[1] * cw0[p]))
 
     for copy in pending:
         copy.wait_send()
@@ -715,18 +797,11 @@
                             part = block[e * ey : (e + 1) * ey]
                             dst[v, (h * group + e) * q + x, pl.ds(y, ey, stride=q), :] = part
 
-    leaving = []
     cnet = Lanes(QC, tile, ez)
     for z in range(QC):
         for a in range(QC * QC):
             tmp_b[a * QC + z] = permuted(ccor[a * QC + z], cnet.place[z])
     write_planes(cresult, tmp_b, QC, cnet)
-    for v in range(QC):
-        copy = pltpu.make_async_copy(
-            cresult.at[v], cor_hbm.at[:, :, v * ez : (v + 1) * ez], cor_sem.at[v]
-        )
-        copy.start()
-        leaving.append(copy)
     for y in range(QC):
         for z in range(QC):
             line = dense(INTERP, [ccor[i * QC * QC + y * QC + z] for i in range(QC)])
@@ -743,23 +818,17 @@
             lifted = dense(INTERP[z : z + 1], [tmp_b[a * QC + i] for i in range(QC)])[0]
             smooth[p] = permuted(smooth[p] + lifted, net.place[z])
     write_planes(result, smooth, QF, net)
-    for v in range(QF):
-        copy = pltpu.make_async_copy(
-            result.at[v], out_hbm.at[:, :, v * ez : (v + 1) * ez], out_sem.at[v]
-        )
-        copy.start()
-        leaving.append(copy)
     for copy in pending:
         copy.wait_send()
-    for copy in leaving:
-        copy.wait()
-
-
-def hand_over(out_ref, cor_ref, out_hbm, cor_hbm, sems):
-    copies = [
-        pltpu.make_async_copy(out_ref, out_hbm, sems.at[0]),
-        pltpu.make_async_copy(cor_ref, cor_hbm, sems.at[1]),
-    ]
+
+
+def hand_over(result, cresult, out_hbm, cor_hbm, out_sem, cor_sem):
+    copies = []
+    for blocks, whole, sems in ((result, out_hbm, out_sem), (cresult, cor_hbm, cor_sem)):
+        count, _, _, ez = blocks.shape
+        for v in range(count):
+            lanes = whole.at[:, :, v * ez : (v + 1) * ez]
+            copies.append(pltpu.make_async_copy(blocks.at[v], lanes, sems.at[v]))
     for copy in copies:
         copy.start()
     for copy in copies:
@@ -778,10 +847,11 @@
     coarse_rows = -(-2 * QC * (QC - 1) * face // 8) * 8
     scratch = [
         pltpu.VMEM((3, QF, px, py, ez), f32),
-        pltpu.VMEM((QF, px, py, ez), f32),
-        pltpu.VMEM((QC, ex * QC, ey * QC, ez), f32),
-        *[pltpu.VMEM((QF**3, subs, ez), f32)] * 10,
-        pltpu.VMEM((14, QC**3, subs, ez), f32),
+        *[pltpu.VMEM((QF**3, subs, ez), f32)] * 8,
+        pltpu.VMEM((3, QF**3, subs, ez), f32),
+        pltpu.VMEM((3, QC**3, subs, ez), f32),
+        *[pltpu.VMEM((QF**3, subs, ez), f32)] * 2,
+        pltpu.VMEM((13, QC**3, subs, ez), f32),
         pltpu.VMEM((QF * QF * QC, subs, ez), f32),
         pltpu.VMEM((QF * QF * QC, subs, ez), f32),
         *[pltpu.VMEM((FINE_STAGES, dirs, fine_rows, ez), f32)] * 2,
@@ -791,8 +861,6 @@
         pltpu.VMEM((2, 8, ez), f32),
         pltpu.VMEM((2, ny, 8, ez), f32),
         pltpu.SemaphoreType.DMA((3, QF)),
-        pltpu.SemaphoreType.DMA((QF,)),
-        pltpu.SemaphoreType.DMA((QC,)),
         pltpu.SemaphoreType.DMA((2, FINE_STAGES, dirs)),
         pltpu.SemaphoreType.DMA((2, COARSE_STAGES, dirs)),
         pltpu.SemaphoreType.DMA((2, 2, longest)),
@@ -803,11 +871,11 @@
     out, cor = pl.pallas_call(
         functools.partial(kernel, nx, ny),
         out_shape=(
-            jax.ShapeDtypeStruct(source.shape, f32),
-            jax.ShapeDtypeStruct((ex * QC, ey * QC, ez * QC), f32),
+            jax.ShapeDtypeStruct((QF, px, py, ez), f32),
+            jax.ShapeDtypeStruct((QC, ex * QC, ey * QC, ez), f32),
         ),
         in_specs=[pl.BlockSpec(memory_space=pltpu.HBM)] * 3,
-        out_specs=(anywhere, anywhere),
+        out_specs=(pl.BlockSpec(memory_space=pltpu.VMEM),) * 2,
         scratch_shapes=scratch,
         compiler_params=pltpu.CompilerParams(
             collective_id=0, has_side_effects=True, vmem_limit_bytes=52 * 1024 * 1024
@@ -815,10 +883,13 @@
     )(source, conductivity, absorption)
     return pl.pallas_call(
         hand_over,
-        out_shape=(out, cor),
+        out_shape=(
+            jax.ShapeDtypeStruct(source.shape, f32),
+            jax.ShapeDtypeStruct((ex * QC, ey * QC, ez * QC), f32),
+        ),
         in_specs=[anywhere] * 2,
         out_specs=(pl.BlockSpec(memory_space=pltpu.HBM),) * 2,
-        scratch_shapes=[pltpu.SemaphoreType.DMA((2,))],
+        scratch_shapes=[pltpu.SemaphoreType.DMA((QF,)), pltpu.SemaphoreType.DMA((QC,))],
         compiler_params=pltpu.CompilerParams(vmem_limit_bytes=1024 * 1024),
     )(out, cor)
 

time: 45.9 us -> 44.2 us (0.963)
  Pallas kernels: 45.1 us -> 43.4 us
    pallas_call x1, Pallas kernels: 43.9 us -> 42.3 us  [on_device(): pl.pallas_call(functools.partial(kernel, nx, ny), out_shape=(jax.ShapeDty...]
where the time goes in v4:
time: 44.2 us; the launch traced here: 44 us
  Pallas kernels  43.4 us (98%)
  between operations  0.64 us (1%)
    pallas_call x1, Pallas kernels, on_device(): pl.pallas_call(functools.partial(kernel, nx, ny), out_shape=(jax.ShapeDty...  42.3 us
    pallas_call x1, Pallas kernels, on_device(): pl.pallas_call(hand_over, out_shape=(jax.ShapeDtypeStruct(source.shape, f...  1.08 us

profile of v4, /device:TPU:0, one launch (start us, length us, event | category | flops | bytes accessed | tf_op | source)
XLA Modules:
  0.0 44.0 jit_solution(15156279795189590228)
XLA Ops:
  0.6 42.3 %shard_map.50 = (f32[5,20,20,128]{3,2,1,0:T(8,128)S(1)}, f32[3,12,12,128]{3,2,1,0:T(8,128)S(1)}) custom-call(f32[20,20,640]{2,1,0:T(8,128)} %src_hbm.1, f32[20,20,640]{2,1,0:T(8,128)} %cond_hbm.1, f32[20,20,640]{2,1,0:T(8,128)} %abs_hbm.1), custom_call_target="tpu_custom_call" | custom-call | tf_op jit(solution)/shard_map/pallas_call | solution.py:871
  42.9 1.1 %shard_map.51 = (f32[20,20,640]{2,1,0:T(8,128)}, f32[12,12,384]{2,1,0:T(8,128)}) custom-call(f32[5,20,20,128]{3,2,1,0:T(8,128)S(1)} %get-tuple-element.4.result, f32[3,12,12,128]{3,2,1,0:T(8,128)S(1)} %get-tuple-element.5.cresult), custom_call_target="tpu_custom_call" | custom-call | tf_op jit(solution)/shard_map/pallas_call | solution.py:884

commit v5 on v4

--- a/solution.py
+++ b/solution.py
@@ -602,8 +602,7 @@
         ends_x = (first_x, last_x) if summed else None
         ends_y = (first_y, last_y) if summed else None
 
-        @pl.loop(0, QF)
-        def _(a):
+        for a in range(QF):
             for c in range(QF):
                 line = [field[i * QF * QF + a * QF + c] for i in range(QF)]
                 line = dense(TRANSFER, weighted(line, ends_x))
@@ -653,6 +652,18 @@
 
     def apply_coarse(src, dst):
         local_op(src, dst, cfluxes, cmass, COARSE_D, lanes)
+
+    def apply_coarse_and_send(src, dst, stage):
+        copies = []
+
+        def first_part():
+            sum_x(dst, QC, inner_c, (0, QC - 1))
+            copies.extend(start_exchange(rough, stage, [(dst, QC)], range(6)))
+
+        local_op(src, dst, cfluxes, cmass, COARSE_D, lanes, first_part)
+        sum_x(dst, QC, inner_c, range(1, QC - 1))
+        sum_y(dst, QC, inner_c)
+        return copies + start_exchange(rough, stage, [(dst, QC)], range(6, len(DIRS)))
 
     keep = lambda p, v: v
     invert = lambda p, v: 1.0 / v
@@ -765,16 +776,12 @@
     first = lambda p, v: cinv[p] * (crhs[p] - scale[2] * v)
     interior(rw2, QC, first)
     finish_exchange(rough, 3, [(rw2, QC)], c_3, [first])
-    apply_coarse(rw2, cw0)
-    local_sum(cw0, QC, inner_c)
-    c_4 = start_exchange(rough, 4, [(cw0, QC)])
+    c_4 = apply_coarse_and_send(rw2, cw0, 4)
     interior(cw0, QC, cscaled)
     cline = start_line(1, False, *finish_line(1, True, cline))
 
     finish_exchange(rough, 4, [(cw0, QC)], c_4, [cscaled])
-    apply_coarse(cw0, cw1)
-    local_sum(cw1, QC, inner_c)
-    c_5 = start_exchange(rough, 5, [(cw1, QC)])
+    c_5 = apply_coarse_and_send(cw0, cw1, 5)
     interior(cw1, QC, cscaled)
     cscale = coefficients(inverse_estimate(*finish_line(1, False, cline)))
     each(QC, store(ccor, lambda p: cscale[0] * rw2[p] + cscale[1] * cw0[p]))

time: 44.2 us -> 44 us (level)
  no operation moved by 1% of the time
where the time goes in v5:
time: 44 us; the launch traced here: 43.8 us
  Pallas kernels  43.2 us (98%)
  between operations  0.64 us (1%)
    pallas_call x1, Pallas kernels, on_device(): pl.pallas_call(functools.partial(kernel, nx, ny), out_shape=(jax.ShapeDty...  42.1 us
    pallas_call x1, Pallas kernels, on_device(): pl.pallas_call(hand_over, out_shape=(jax.ShapeDtypeStruct(source.shape, f...  1.08 us

profile of v5, /device:TPU:0, one launch (start us, length us, event | category | flops | bytes accessed | tf_op | source)
XLA Modules:
  0.0 43.8 jit_solution(13904295338874849792)
XLA Ops:
  0.6 42.1 %shard_map.50 = (f32[5,20,20,128]{3,2,1,0:T(8,128)S(1)}, f32[3,12,12,128]{3,2,1,0:T(8,128)S(1)}) custom-call(f32[20,20,640]{2,1,0:T(8,128)} %src_hbm.1, f32[20,20,640]{2,1,0:T(8,128)} %cond_hbm.1, f32[20,20,640]{2,1,0:T(8,128)} %abs_hbm.1), custom_call_target="tpu_custom_call" | custom-call | tf_op jit(solution)/shard_map/pallas_call | solution.py:878
  42.7 1.1 %shard_map.51 = (f32[20,20,640]{2,1,0:T(8,128)}, f32[12,12,384]{2,1,0:T(8,128)}) custom-call(f32[5,20,20,128]{3,2,1,0:T(8,128)S(1)} %get-tuple-element.4.result, f32[3,12,12,128]{3,2,1,0:T(8,128)S(1)} %get-tuple-element.5.cresult), custom_call_target="tpu_custom_call" | custom-call | tf_op jit(solution)/shard_map/pallas_call | solution.py:891
